TPU v7x, 32 devices: a whole 2x2x4 slice. The times are simulated.
32 devices in a mesh: rel: 4 (over x, core), dst: 4 (over z), mp: 2 (over y).
Axes of the slice: x: 2, y: 2, z: 4, core: 2. Of those that a mesh axis runs over, the one named last changes fastest.
Arguments:
- node_table: bfloat16 [16384, 512], P(('rel', 'dst')), may hold values from -6 to 6
- edge_weights: bfloat16 [4, 32, 128, 128], P('rel', 'dst'), may hold values from -0.5 to 0.5
- src_ids: int32 [4, 32, 128], P('rel', 'dst'), may hold values from 0 to 1023
- dst_ids: int32 [4, 32, 128], P('rel', 'dst'), may hold values from 0 to 511
- block_mask: int32 [4, 32], P('rel', 'dst'), may hold values 0 or 1
- basis_coef: float32 [4, 32], P('rel'), may hold values from -0.375 to 0.375
- basis_mats: bfloat16 [32, 512, 512], P(None, None, 'mp'), may hold values from -0.25 to 0.25
- type_bias: float32 [4, 512], P(None, 'mp'), may hold values from -3 to 3
- type_rows: int32 [4], replicated, may hold values from 1 to 256, 512 in all
- cotangent: bfloat16 [2048, 512], P(('rel', 'dst'), 'mp'), may hold values from -0.005859375 to 0.005859375
Outputs:
- layer_out: bfloat16 [2048, 512], P(('rel', 'dst'), 'mp')
- coef_grad: float32 [4, 32], P('rel')
Inputs may be any that keep to these rules, and one draw needn't show every extreme that they name: `type_rows`: the 4 counts sum to 512.
All inputs are finite; a program needn't handle non-finite values. No bound on the sum of `block_mask` on one device may be relied on, other than what follows from the above.
Results may differ from a plain program's by a relative error of at most 0.0062.
Values may be sent and summed in bfloat16 or wider, within the bound.
No kernel may reach another device: no remote copies, remote signals or barrier semaphores. Data moves between devices by JAX's collectives and lax.ppermute only.
A program may use at most 64 MiB of HBM per device.

v0:
```python
import jax
import jax.numpy as jnp
from jax import lax
from jax.sharding import PartitionSpec as P

highest = lax.Precision.HIGHEST


def on_device(
    node_table,
    edge_weights,
    src_ids,
    dst_ids,
    block_mask,
    basis_coef,
    basis_mats,
    type_bias,
    type_rows,
    cotangent,
):
    features = node_table.shape[1]
    out_cols = basis_mats.shape[2]
    basis_count = basis_mats.shape[0]
    block_count = edge_weights.shape[1]
    block_rows = edge_weights.shape[2]
    local_rows = cotangent.shape[0]
    owner_span = local_rows * lax.axis_size("rel")
    contract_rows = (((0,), (0,)), ((), ()))
    picked = jnp.take(node_table, src_ids[0].reshape(-1), axis=0).reshape(
        block_count, block_rows, features
    )
    scaled = edge_weights[0] * block_mask[0][:, None, None].astype(jnp.bfloat16)
    messages = jnp.einsum(
        "kij,kjf->kif", scaled, picked, preferred_element_type=jnp.float32
    ).astype(jnp.bfloat16)
    basis_flat = basis_mats.reshape(basis_count, -1)
    mixing = jnp.dot(basis_coef[0], basis_flat, precision=highest)
    weight = mixing.reshape(features, out_cols).astype(jnp.bfloat16)
    owner_grad = lax.all_gather(cotangent, "rel", axis=0, tiled=True)
    slot_local = dst_ids[0]
    arrived, arrived_ids = (
        lax.all_to_all(messages, "dst", split_axis=0, concat_axis=0, tiled=True),
        lax.all_to_all(slot_local, "dst", split_axis=0, concat_axis=0, tiled=True),
    )
    flat_rows = arrived.reshape(-1, features)
    outgoing = jnp.dot(flat_rows, weight, preferred_element_type=jnp.float32).astype(jnp.bfloat16)
    selector = (
        jnp.arange(owner_span, dtype=jnp.int32)[:, None] == arrived_ids.reshape(1, -1)
    ).astype(jnp.bfloat16)
    summed = jnp.dot(selector, outgoing, preferred_element_type=jnp.float32)
    wanted = lax.dot_general(
        selector, owner_grad, contract_rows, preferred_element_type=jnp.float32
    ).astype(jnp.bfloat16)
    outer_sum = lax.dot_general(
        flat_rows, wanted, contract_rows, preferred_element_type=jnp.float32
    )
    relation_total = lax.psum_scatter(summed, "rel", scatter_dimension=0, tiled=True)
    position = lax.axis_index("rel") * local_rows + jnp.arange(local_rows, dtype=jnp.int32)
    bounds = jnp.cumsum(type_rows)
    row_kind = jnp.sum((position[:, None] >= bounds[None, :]).astype(jnp.int32), axis=1)
    kind_table = (
        row_kind[:, None] == jnp.arange(type_rows.shape[0], dtype=jnp.int32)[None, :]
    ).astype(jnp.float32)
    row_bias = jnp.dot(kind_table, type_bias, precision=highest)
    layer_out = (relation_total + row_bias).astype(jnp.bfloat16)
    partial_value = jnp.dot(basis_flat, outer_sum.reshape(-1), precision=highest)
    basis_grads = lax.psum(partial_value, ("dst", "mp"))
    return (layer_out, basis_grads[None, :])


def solution(mesh):
    in_specs = (
        P(("rel", "dst"), None),
        P("rel", "dst", None, None),
        P("rel", "dst", None),
        P("rel", "dst", None),
        P("rel", "dst"),
        P("rel", None),
        P(None, None, "mp"),
        P(None, "mp"),
        P(),
        P(("rel", "dst"), "mp"),
    )
    out_specs = (P(("rel", "dst"), "mp"), P("rel", None))
    return jax.shard_map(
        on_device, mesh=mesh, in_specs=in_specs, out_specs=out_specs, check_vma=False
    )
```

profile of v0, /device:TPU:0, one launch (start us, length us, event | category | flops | bytes accessed | tf_op | source)
XLA Modules:
  0.0 98.5 jit_solution(5001905134119328474)
XLA Ops:
  7.2 0.0 copy-start
  7.2 0.0 copy-start.1
  7.2 0.0 copy-start.2
  7.2 0.0 copy-start.4
  7.2 6.5 %all-to-all-start = ((s32[4,2,128]{2,1,0:T(2,128)}), s32[4,2,128]{2,1,0:T(2,128)S(1)}, u32[]{:S(2)}, u32[]{:S(2)}) async-start(s32[4,2,128]{2,1,0:T(2,128)} %bitcast.52), calls=%async_computation | async-start | bytes 8192 | tf_op jit(solution)/shard_map/all_to_all | solution.py:43
  13.7 0.7 compare_and_fusion
  14.4 0.7 compare_select_fusion
  15.1 0.7 convert_bitcast_fusion
  15.8 0.0 copy-done
  15.8 4.0 %gather_fusion = bf16[1024,512]{1,0:T(8,128)(2,1)S(1)} fusion(bf16[1024,512]{1,0:T(8,128)(2,1)S(1)} %copy-done, s32[1024]{0:T(1024)S(1)} %broadcast_clamp_fusion), kind=kCustom, calls=%fused_computation | custom fusion | bytes 2101248 | tf_op jit(solution)/shard_map/jit(_take)/gather | solution.py:29
  19.7 0.0 copy-done.1
  19.7 1.5 %convolution_convert_fusion = bf16[8,128,512]{2,1,0:T(8,128)(2,1)} fusion(bf16[8,128,512]{2,1,0:T(8,128)(2,1)S(1)} %bitcast.47, pred[8,128]{1,0:T(8,128)(4,1)S(1)} %compare_and_fusion, bf16[1,8,128,128]{3,2,1,0:T(8,128)(2,1)S(1)} %copy-done.1, bf16[8]{0:T(256)(128)(2,1)S(1)} %convert_bitcast_fusion), kind=kOutput, calls=%fused_computation.9 | convolution fusion | flops 135397376 | bytes 2360336 | tf_op jit(solution)/shard_map/kij,kjf->kif/dot_general | solution.py:33
  21.2 0.0 all-to-all-done
  21.2 5.1 %all-to-all-start.1 = ((bf16[8,128,512]{2,1,0:T(8,128)(2,1)}), bf16[8,128,512]{2,1,0:T(8,128)(2,1)S(1)}, u32[]{:S(2)}, u32[]{:S(2)}) async-start(bf16[8,128,512]{2,1,0:T(8,128)(2,1)} %convolution_convert_fusion), calls=%async_computation.1 | async-start | bytes 2097152 | tf_op jit(solution)/shard_map/all_to_all | solution.py:42
  26.3 0.0 copy-start.5
  26.3 0.0 reduce-scatter.2.cloned.1.call-start
  26.3 0.0 copy-done.2
  26.3 5.8 %all_gather.3 = bf16[512,256]{1,0:T(8,128)(2,1)S(1)} all-gather(bf16[128,256]{1,0:T(8,128)(2,1)S(1)} %copy-done.2), channel_id=1, replica_groups=mesh['rel'=4,'dst'=4,'mp'=2] {'rel'}, dimensions={0}, use_global_device_ids=true | all-gather | bytes 327680 | tf_op jit(solution)/shard_map/all_gather | solution.py:39
  32.1 0.0 copy-done.4
  32.1 11.5 %fusion = bf16[1,512,256]{2,0,1:T(2,128)(2,1)S(1)} fusion(f32[1,32]{1,0:T(1,128)S(1)} %copy-done.4, bf16[4,8,512,256]{3,2,1,0:T(8,128)(2,1)} %bitcast.55), kind=kOutput, calls=%fused_computation.1 | convolution fusion | flops 50331648 | bytes 8650880 | tf_op jit(solution)/shard_map/dot_general | solution.py:37
  43.6 7.9 %all-to-all-done.1 = bf16[8,128,512]{2,1,0:T(8,128)(2,1)S(1)} async-done(((bf16[8,128,512]{2,1,0:T(8,128)(2,1)}), bf16[8,128,512]{2,1,0:T(8,128)(2,1)S(1)}, u32[]{:S(2)}, u32[]{:S(2)}) %all-to-all-start.1) | async-done | bytes 1048608 | tf_op jit(solution)/shard_map/all_to_all | solution.py:42
  51.5 0.0 copy-start.3
  51.5 1.9 %fusion.6 = f32[512,256]{1,0:T(8,128)} fusion(bf16[1024,512]{1,0:T(8,128)(2,1)S(1)} %bitcast.48, s32[1024]{0:T(1024)S(1)} %bitcast.53, bf16[1,512,256]{2,0,1:T(2,128)(2,1)S(1)} %fusion), kind=kOutput, calls=%fused_computation.8 | convolution fusion | flops 537657344 | bytes 1839104 | tf_op jit(solution)/shard_map/dot_general | solution.py:50
  53.4 0.0 reduce-scatter.2.cloned.1.call-update
  53.4 0.0 copy-done.5
  53.4 0.2 reduce-window.8
  53.6 0.1 convert_reduce_fusion
  53.7 1.2 %fusion.9 = f32[512,256,1]{1,0,2:T(8,128)S(1)} fusion(bf16[1024,512]{1,0:T(8,128)(2,1)S(1)} %bitcast.49, bf16[512,256]{1,0:T(8,128)(2,1)S(1)} %all_gather.3, s32[1024]{0:T(1024)S(1)} %bitcast.54), kind=kOutput, calls=%fused_computation.13 | convolution fusion | flops 537657344 | bytes 1839104 | tf_op jit(solution)/shard_map/dot_general | solution.py:54
  54.9 14.9 %fusion.11 = f32[1,32]{1,0:T(1,128)S(1)} fusion(bf16[32,512,256]{2,1,0:T(8,128)(2,1)} %param.16, f32[512,256,1]{1,0,2:T(8,128)S(1)} %fusion.9), kind=kOutput, calls=%fused_computation.16 | convolution fusion | flops 50331648 | bytes 8913024 | tf_op jit(solution)/shard_map/dot_general | solution.py:66
  69.8 20.0 %psum.7 = f32[1,32]{1,0:T(1,128)} all-reduce(f32[1,32]{1,0:T(1,128)S(1)} %fusion.11), channel_id=1, replica_groups=mesh['rel'=4,'dst'=4,'mp'=2] {'dst','mp'}, use_global_device_ids=true, to_apply=%region_3.4 | all-reduce | flops 32 | bytes 256 | tf_op jit(solution)/shard_map/psum | solution.py:67
  89.9 0.0 copy-done.3
  89.9 1.8 %fusion.10 = bf16[128,256]{1,0:T(8,128)(2,1)} fusion(f32[128,256]{1,0:T(8,128)} %reduce-scatter.2.cloned.1.call-done, f32[4,256]{1,0:T(4,128)S(1)} %copy-done.3, s32[128]{0:T(128)S(1)} %convert_reduce_fusion), kind=kOutput, calls=%fused_computation.15 | convolution fusion | flops 1638912 | bytes 201216 | tf_op jit(solution)/shard_map/dot_general | solution.py:64
  (3 shorter events, 0.0 us)
Async XLA Ops:
  7.2 8.6 %copy-start = (bf16[1024,512]{1,0:T(8,128)(2,1)S(1)}, bf16[1024,512]{1,0:T(8,128)(2,1)}, u32[]{:S(2)}) copy-start(bf16[1024,512]{1,0:T(8,128)(2,1)} %param.10) | copy-start | bytes 3145732
  7.2 12.5 %copy-start.1 = (bf16[1,8,128,128]{3,2,1,0:T(8,128)(2,1)S(1)}, bf16[1,8,128,128]{3,2,1,0:T(8,128)(2,1)}, u32[]{:S(2)}) copy-start(bf16[1,8,128,128]{3,2,1,0:T(8,128)(2,1)} %param.11) | copy-start | bytes 786436
  7.2 19.1 %copy-start.2 = (bf16[128,256]{1,0:T(8,128)(2,1)S(1)}, bf16[128,256]{1,0:T(8,128)(2,1)}, u32[]{:S(2)}) copy-start(bf16[128,256]{1,0:T(8,128)(2,1)} %param.19) | copy-start | bytes 196612
  7.2 24.9 %copy-start.4 = (f32[1,32]{1,0:T(1,128)S(1)}, f32[1,32]{1,0:T(1,128)}, u32[]{:S(2)}) copy-start(f32[1,32]{1,0:T(1,128)} %param.15) | copy-start | bytes 388
  7.2 14.0 %all-to-all-start = ((s32[4,2,128]{2,1,0:T(2,128)}), s32[4,2,128]{2,1,0:T(2,128)S(1)}, u32[]{:S(2)}, u32[]{:S(2)}) async-start(s32[4,2,128]{2,1,0:T(2,128)} %bitcast.52), calls=%async_computation | async-start | bytes 8192 | tf_op jit(solution)/shard_map/all_to_all | solution.py:43
  21.2 30.3 %all-to-all-start.1 = ((bf16[8,128,512]{2,1,0:T(8,128)(2,1)}), bf16[8,128,512]{2,1,0:T(8,128)(2,1)S(1)}, u32[]{:S(2)}, u32[]{:S(2)}) async-start(bf16[8,128,512]{2,1,0:T(8,128)(2,1)} %convolution_convert_fusion), calls=%async_computation.1 | async-start | bytes 2097152 | tf_op jit(solution)/shard_map/all_to_all | solution.py:42
  26.3 27.1 %copy-start.5 = (s32[4]{0:T(128)S(1)}, s32[4]{0:T(128)}, u32[]{:S(2)}) copy-start(s32[4]{0:T(128)} %param.18) | copy-start | bytes 52
  26.3 63.6 %reduce-scatter.2.cloned.1.call-start = ((), (), s32[]{:S(2)}) async-start(), calls=%async_computation.3 | async-start | bytes 655360 | tf_op jit(solution)/shard_map/reduce_scatter | solution.py:57
  51.5 38.4 %copy-start.3 = (f32[4,256]{1,0:T(4,128)S(1)}, f32[4,256]{1,0:T(4,128)}, u32[]{:S(2)}) copy-start(f32[4,256]{1,0:T(4,128)} %param.17) | copy-start | bytes 12292
Sparse Core Ops, SparseCore 0:
  53.5 20.7 reduce-scatter.1
where the time goes:
time: 98.9 us; the launch traced here: 98.5 us
  matrix products  32.8 us (33%)
  blocking collectives  25.8 us (26%)
  between operations  14.1 us (14%)
  starting transfers between devices  11.6 us (12%)
  waiting for transfers between devices  7.93 us (8%)
  local copies, waits for them, and re-layouts  3.99 us (4%)
  other arithmetic  2.32 us (2%)
    psum x1, blocking collectives, on_device(): basis_grads = lax.psum(partial_value, ('dst', 'mp'))  20 us
    dot_general x1, matrix products, on_device(): jnp.dot(basis_flat, outer_sum.reshape(-1), precision=highest)  14.9 us
    dot_general x1, matrix products, on_device(): mixing = jnp.dot(basis_coef[0], basis_flat, precision=highest)  11.5 us
    all_to_all x1, waiting for transfers between devices, on_device(): lax.all_to_all(messages, 'dst', split_axis=0, concat_axis=0, tiled=True)  7.91 us
    all_to_all x1, starting transfers between devices, on_device(): lax.all_to_all(slot_local, 'dst', split_axis=0, concat_axis=0, tiled=True)  6.49 us
    all_gather x1, blocking collectives, on_device(): owner_grad = lax.all_gather(cotangent, 'rel', axis=0, tiled=True)  5.78 us
    all_to_all x1, starting transfers between devices, on_device(): lax.all_to_all(messages, 'dst', split_axis=0, concat_axis=0, tiled=True)  5.09 us
    gather x1, local copies, waits for them, and re-layouts, on_device(): jnp.take(node_table, src_ids[0].reshape(-1), axis=0)  3.96 us
  transfers between devices with their start and end apart: 3, of which 1 were waited for; matrix products, arithmetic and copies ran while one was open for 36% of the time, Pallas kernels for 0%

commit v1 on v0

v1 whole, which is shorter than its diff:
```python
import functools
import jax
import jax.numpy as jnp
from jax import lax
from jax.experimental import pallas as pl
from jax.experimental.pallas import tpu as pltpu
from jax.sharding import PartitionSpec as P

f32, bf16, i32 = jnp.float32, jnp.bfloat16, jnp.int32
LIMIT = 40 * 1024 * 1024
CONTRACT_ROWS = (((0,), (0,)), ((), ()))


def whole(space=pltpu.VMEM):
    return pl.BlockSpec(memory_space=space)


def swap(x, axis, d):
    n = lax.axis_size(axis)
    return lax.ppermute(x, axis, [(i, i ^ d) for i in range(n)])


def spread_rows(row, rows):
    return jnp.broadcast_to(row, (rows, rows)).T


def one_hot(column, width):
    rows, lanes = column.shape
    lane = lax.broadcasted_iota(i32, (rows, lanes), 1)
    parts = [(column == lane + c).astype(bf16) for c in range(0, width, lanes)]
    return jnp.concatenate(parts, axis=1)


def send_kernel(
    n_dst, coef, mask, src, dst, table, weights, basis, messages, *rest
):
    outs, acc = rest[:n_dst], rest[n_dst]
    step, steps = pl.program_id(0), pl.num_programs(0)
    per_step, features, cols = basis.shape
    block = weights.shape[-1]
    blocks = src.shape[1]
    per_owner = blocks // n_dst

    column = spread_rows(src[0, pl.ds(step, 1), :], block)
    picked = jnp.dot(
        one_hot(column, table.shape[0]), table[...], preferred_element_type=f32
    ).astype(bf16)
    scaled = weights[0, 0] * mask[0, step].astype(f32).astype(bf16)
    rows = pl.ds(pl.multiple_of(step * block, block), block)
    messages[rows, :] = jnp.dot(scaled, picked, preferred_element_type=f32).astype(bf16)

    factors = [coef[0, step * per_step + b] for b in range(per_step)]
    chunk = 64
    for start in range(0, features, chunk):
        part = pl.ds(start, chunk)
        total = factors[0] * basis[0, part, :].astype(f32)
        for b in range(1, per_step):
            total = total + factors[b] * basis[b, part, :].astype(f32)

        @pl.when(step == 0)
        def _():
            acc[part, :] = total

        @pl.when(step > 0)
        def _():
            acc[part, :] = acc[part, :] + total

    @pl.when(step == steps - 1)
    def _():
        weight = acc[...].astype(bf16)
        me = lax.axis_index("dst")
        span = per_owner * block
        for d in range(n_dst):
            owner = me ^ d
            mine = messages[pl.ds(pl.multiple_of(owner * span, span), span), :]
            outs[d][:span, :] = jnp.dot(mine, weight, preferred_element_type=f32).astype(bf16)
            pad = outs[d].shape[0] - span
            which = lax.broadcasted_iota(i32, (pad, block), 0)
            slots = jnp.zeros((pad, block), i32)
            for b in range(per_owner):
                ids = dst[0, pl.ds(owner * per_owner + b, 1), :]
                slots = jnp.where(which == 2 * b, ids & 255, slots)
                slots = jnp.where(which == 2 * b + 1, ids >> 8, slots)
            outs[d][span:, :block] = slots.astype(f32).astype(bf16)
            outs[d][span:, block:] = jnp.zeros((pad, cols - block), bf16)


def send(coef, mask, src, dst, table, weights, basis, n_dst):
    count, features, cols = basis.shape
    blocks, block = src.shape[1:]
    per_step = count // blocks
    span = blocks // n_dst * block
    pad = -(-2 * (blocks // n_dst) // 16) * 16
    smem = pl.BlockSpec(memory_space=pltpu.SMEM)
    return pl.pallas_call(
        functools.partial(send_kernel, n_dst),
        grid=(blocks,),
        in_specs=[
            smem,
            smem,
            whole(),
            whole(),
            whole(),
            pl.BlockSpec((1, 1, block, block), lambda k: (0, k, 0, 0)),
            pl.BlockSpec((per_step, features, cols), lambda k: (k, 0, 0)),
        ],
        out_shape=[jax.ShapeDtypeStruct((blocks * block, features), bf16)]
        + [jax.ShapeDtypeStruct((span + pad, cols), bf16)] * n_dst,
        out_specs=[whole()] * (1 + n_dst),
        scratch_shapes=[pltpu.VMEM((features, cols), f32)],
        compiler_params=pltpu.CompilerParams(
            dimension_semantics=("arbitrary",), vmem_limit_bytes=LIMIT
        ),
        cost_estimate=pl.CostEstimate(flops=6_000_000_000, bytes_accessed=10_000_000, transcendentals=0),
        name="send",
    )(coef, mask, src, dst, table, weights, basis)


def grad_kernel(n_rel, n_dst, dst, messages, basis, *rest):
    pieces, out = rest[: n_rel * n_dst], rest[n_rel * n_dst]
    table, outer, sums = rest[n_rel * n_dst + 1 :]
    step, steps = pl.program_id(0), pl.num_programs(0)
    per_step, features, cols = basis.shape
    blocks, block = dst.shape[1:]
    rows_dev = pieces[0].shape[0]
    per_owner = blocks // n_dst
    span = per_owner * block
    owner_rows = n_rel * rows_dev

    @pl.when(step == 0)
    def _():
        rel, me = lax.axis_index("rel"), lax.axis_index("dst")
        for d in range(n_dst):
            for e in range(n_rel):
                at = (me ^ d) * owner_rows + (rel ^ e) * rows_dev
                table[pl.ds(pl.multiple_of(at, rows_dev), rows_dev), :] = pieces[
                    d * n_rel + e
                ][...]
        total = jnp.zeros((features, cols), f32)
        for o in range(n_dst):
            own = table[o * owner_rows : (o + 1) * owner_rows, :]
            parts = []
            for b in range(per_owner):
                k = o * per_owner + b
                column = spread_rows(dst[0, k : k + 1, :], block)
                parts.append(one_hot(column, owner_rows))
            picks = jnp.concatenate(parts, axis=0)
            wanted = jnp.dot(picks, own, preferred_element_type=f32).astype(bf16)
            total = total + lax.dot_general(
                messages[o * span : (o + 1) * span, :],
                wanted,
                CONTRACT_ROWS,
                preferred_element_type=f32,
            )
        outer[...] = total

    for b in range(per_step):
        total = jnp.zeros((8, 128), f32)
        for start in range(0, features, 32):
            part = pl.ds(start, 32)
            prod = basis[b, part, :].astype(f32) * outer[part, :]
            for r in range(0, 32, 8):
                for c in range(0, cols, 128):
                    total = total + prod[r : r + 8, c : c + 128]
        sums[pl.ds(step * per_step + b, 1), :] = jnp.sum(total, axis=0, keepdims=True)

    @pl.when(step == steps - 1)
    def _():
        out[...] = jnp.sum(sums[...].T, axis=0, keepdims=True)


def grad(dst, messages, basis, pieces, n_rel, n_dst):
    count, features, cols = basis.shape
    blocks = dst.shape[1]
    per_step = count // 8
    rows_dev = pieces[0].shape[0]
    return pl.pallas_call(
        functools.partial(grad_kernel, n_rel, n_dst),
        grid=(8,),
        in_specs=[
            whole(),
            whole(),
            pl.BlockSpec((per_step, features, cols), lambda k: (k, 0, 0)),
        ]
        + [whole()] * len(pieces),
        out_shape=jax.ShapeDtypeStruct((1, 128), f32),
        out_specs=whole(),
        scratch_shapes=[
            pltpu.VMEM((n_dst * n_rel * rows_dev, cols), bf16),
            pltpu.VMEM((features, cols), f32),
            pltpu.VMEM((128, 128), f32),
        ],
        compiler_params=pltpu.CompilerParams(
            dimension_semantics=("arbitrary",), vmem_limit_bytes=LIMIT
        ),
        cost_estimate=pl.CostEstimate(flops=4_000_000_000, bytes_accessed=10_000_000, transcendentals=0),
        name="grad",
    )(dst, messages, basis, *pieces)


def gather_kernel(n_rel, n_dst, block, *refs):
    got, outs = refs[:n_dst], refs[n_dst:]
    rows_dev = outs[0].shape[0]
    span = got[0].shape[0] // block * block
    rel = lax.axis_index("rel")
    ids = []
    for d in range(n_dst):
        pairs = got[d][span:, :block].astype(f32)
        ids.append(
            [
                (pairs[2 * b : 2 * b + 1] + 256.0 * pairs[2 * b + 1 : 2 * b + 2]).astype(i32)
                for b in range(span // block)
            ]
        )
    row = lax.broadcasted_iota(i32, (rows_dev, block), 0)
    for e in range(n_rel):
        place = row + (rel ^ e) * rows_dev
        total = None
        for d in range(n_dst):
            picks = jnp.concatenate(
                [(place == one).astype(bf16) for one in ids[d]], axis=1
            )
            more = jnp.dot(picks, got[d][:span, :], preferred_element_type=f32)
            total = more if total is None else total + more
        outs[e][...] = total.astype(outs[e].dtype)


def gather(got, n_rel, block, rows_dev):
    n_dst, cols = len(got), got[0].shape[1]
    return pl.pallas_call(
        functools.partial(gather_kernel, n_rel, n_dst, block),
        in_specs=[whole()] * n_dst,
        out_shape=[
            jax.ShapeDtypeStruct((rows_dev, cols), f32 if e == 0 else bf16)
            for e in range(n_rel)
        ],
        out_specs=[whole()] * n_rel,
        compiler_params=pltpu.CompilerParams(vmem_limit_bytes=LIMIT),
        cost_estimate=pl.CostEstimate(flops=600_000_000, bytes_accessed=1_000_000, transcendentals=0),
        name="gather",
    )(*got)


def finish_kernel(type_rows, bias, *refs):
    parts, out = refs[:-1], refs[-1]
    rows_dev, cols = out.shape
    kinds = bias.shape[0]
    total = parts[0][...]
    for part in parts[1:]:
        total = total + part[...].astype(f32)
    first = lax.axis_index("rel") * rows_dev
    row = lax.broadcasted_iota(i32, (rows_dev, cols), 0) + first
    added = jnp.broadcast_to(bias[0:1, :], (rows_dev, cols))
    bound = 0
    for c in range(kinds - 1):
        bound = bound + type_rows[c]
        added = jnp.where(row >= bound, bias[c + 1 : c + 2, :], added)
    out[...] = (total + added).astype(out.dtype)


def finish(type_rows, bias, parts):
    return pl.pallas_call(
        finish_kernel,
        in_specs=[whole(pltpu.SMEM), whole()] + [whole()] * len(parts),
        out_shape=jax.ShapeDtypeStruct(parts[0].shape, bf16),
        out_specs=whole(),
        compiler_params=pltpu.CompilerParams(vmem_limit_bytes=LIMIT),
        name="finish",
    )(type_rows, bias, *parts)


def on_device(
    node_table,
    edge_weights,
    src_ids,
    dst_ids,
    block_mask,
    basis_coef,
    basis_mats,
    type_bias,
    type_rows,
    cotangent,
):
    n_rel, n_dst, n_mp = (lax.axis_size(a) for a in ("rel", "dst", "mp"))
    block = edge_weights.shape[-1]
    rows_dev = cotangent.shape[0]

    along = [cotangent] + [swap(cotangent, "dst", d) for d in range(1, n_dst)]
    grid = [[piece] for piece in along]
    for e in range(2, n_rel, 2):
        for d in range(n_dst):
            grid[d].append(swap(along[d], "rel", e))
    pieces = []
    for d in range(n_dst):
        for mine in grid[d]:
            pieces += [mine, swap(mine, "rel", 1)]

    messages, *queues = send(
        basis_coef, block_mask, src_ids, dst_ids, node_table, edge_weights, basis_mats, n_dst
    )
    got = [queues[0]] + [swap(queues[d], "dst", d) for d in range(1, n_dst)]
    sums = gather(got, n_rel, block, rows_dev)
    parts = [sums[0]] + [swap(sums[e], "rel", e) for e in range(1, n_rel)]
    layer_out = finish(type_rows, type_bias, parts)

    partial = grad(dst_ids, messages, basis_mats, pieces, n_rel, n_dst)
    for axis, size in (("mp", n_mp), ("dst", n_dst)):
        d = 1
        while d < size:
            partial = partial + swap(partial, axis, d)
            d *= 2
    return layer_out, partial[:, : basis_coef.shape[1]]


def solution(mesh):
    in_specs = (
        P(("rel", "dst"), None),
        P("rel", "dst", None, None),
        P("rel", "dst", None),
        P("rel", "dst", None),
        P("rel", "dst"),
        P("rel", None),
        P(None, None, "mp"),
        P(None, "mp"),
        P(),
        P(("rel", "dst"), "mp"),
    )
    out_specs = (P(("rel", "dst"), "mp"), P("rel", None))
    return jax.shard_map(
        on_device, mesh=mesh, in_specs=in_specs, out_specs=out_specs, check_vma=False
    )
```

time: 98.9 us -> 59.2 us (0.60)
  matrix products: 32.8 us -> 0 us
  blocking collectives: 25.8 us -> 0 us
  between operations: 14.1 us -> 0.75 us
  Pallas kernels: 0 us -> 12.4 us
  starting transfers between devices: 11.6 us -> 23.4 us
  waiting for transfers between devices: 7.93 us -> 13.6 us
  local copies, waits for them, and re-layouts: 3.99 us -> 8.25 us
  other arithmetic: 2.32 us -> 0.52 us
    dot_general x6 -> x0, matrix products: 32.8 us -> none  [the longest x1 14.9 us: on_device(): jnp.dot(basis_flat, outer_sum.reshape(-1), precision=highest)]
    ppermute x0 -> x24, starting transfers between devices: none -> 23.4 us  [swap(): return lax.ppermute(x, axis, [(i, i ^ d) for i in range(n)])]
    psum x1 -> x0, blocking collectives: 20 us -> none  [on_device(): basis_grads = lax.psum(partial_value, ('dst', 'mp'))]
    ppermute x0 -> x24, waiting for transfers between devices: none -> 13.6 us  [swap(): return lax.ppermute(x, axis, [(i, i ^ d) for i in range(n)])]
    pallas_call x0 -> x4, Pallas kernels: none -> 12.4 us  [the longest x1 7.08 us: send(): pl.pallas_call(functools.partial(send_kernel, n_dst), grid=(blocks,), in_...]
    all_to_all x2 -> x0, starting transfers between devices: 11.6 us -> none  [the longest x1 6.49 us: on_device(): lax.all_to_all(slot_local, 'dst', split_axis=0, concat_axis=0, tiled=True)]
    unnamed x12 -> x24, local copies, waits for them, and re-layouts: 0.03 us -> 8.25 us
    all_to_all x2 -> x0, waiting for transfers between devices: 7.92 us -> none  [the longest x1 7.91 us: on_device(): lax.all_to_all(messages, 'dst', split_axis=0, concat_axis=0, tiled=True)]
  transfers between devices with their start and end apart: 3 -> 24, of which waited for: 1 -> 8; matrix products, arithmetic and copies ran while one was open for 36% -> 1% of each run, Pallas kernels for 0% -> 7%
where the time goes in v1:
time: 59.2 us; the launch traced here: 58.9 us
  starting transfers between devices  23.4 us (40%)
  waiting for transfers between devices  13.6 us (23%)
  Pallas kernels  12.4 us (21%)
  local copies, waits for them, and re-layouts  8.25 us (14%)
  between operations  0.75 us (1%)
    ppermute x24, starting transfers between devices, swap(): return lax.ppermute(x, axis, [(i, i ^ d) for i in range(n)])  23.4 us
    ppermute x24, waiting for transfers between devices, swap(): return lax.ppermute(x, axis, [(i, i ^ d) for i in range(n)])  13.6 us
    unnamed x24, local copies, waits for them, and re-layouts  8.25 us
    pallas_call x1, Pallas kernels, send(): pl.pallas_call(functools.partial(send_kernel, n_dst), grid=(blocks,), in_...  7.08 us
    pallas_call x1, Pallas kernels, grad(): pl.pallas_call(functools.partial(grad_kernel, n_rel, n_dst), grid=(8,), i...  3.6 us
    pallas_call x1, Pallas kernels, finish(): pl.pallas_call(finish_kernel, in_specs=[whole(pltpu.SMEM), whole()] + [wh...  1.23 us
  transfers between devices with their start and end apart: 24, of which 8 were waited for; matrix products, arithmetic and copies ran while one was open for 1% of the time, Pallas kernels for 7%

profile of v1, /device:TPU:0, one launch (start us, length us, event | category | flops | bytes accessed | tf_op | source)
XLA Modules:
  0.0 58.9 jit_solution(3909933998291966991)
XLA Ops:
  0.6 3.0 %collective-permute-start.7 = (bf16[128,256]{1,0:T(8,128)(2,1)}, bf16[128,256]{1,0:T(8,128)(2,1)S(1)}, u32[]{:S(2)}, u32[]{:S(2)}) collective-permute-start(bf16[128,256]{1,0:T(8,128)(2,1)} %rest_0_.1), channel_id=1, source_target_pairs={{0,16},{8,24},{16,0},{24,8},{1,17},{9,25},{17,1},{25,9},{2,18},{10... | collective-permute-start | bytes 196616 | tf_op jit(solution)/shard_map/ppermute | solution.py:20
  3.7 1.6 %collective-permute-start.9 = (bf16[128,256]{1,0:T(8,128)(2,1)}, bf16[128,256]{1,0:T(8,128)(2,1)S(1)}, u32[]{:S(2)}, u32[]{:S(2)}) collective-permute-start(bf16[128,256]{1,0:T(8,128)(2,1)} %rest_0_.1), channel_id=1, source_target_pairs={{0,2},{2,0},{4,6},{6,4},{1,3},{3,1},{5,7},{7,5},{8,10},{10,8},{12,... | collective-permute-start | bytes 196616 | tf_op jit(solution)/shard_map/ppermute | solution.py:20
  5.2 2.6 %collective-permute-start.13 = (bf16[128,256]{1,0:T(8,128)(2,1)}, bf16[128,256]{1,0:T(8,128)(2,1)S(1)}, u32[]{:S(2)}, u32[]{:S(2)}) collective-permute-start(bf16[128,256]{1,0:T(8,128)(2,1)} %rest_0_.1), channel_id=1, source_target_pairs={{0,4},{2,6},{4,0},{6,2},{1,5},{3,7},{5,1},{7,3},{8,12},{10,14},{12... | collective-permute-start | bytes 196616 | tf_op jit(solution)/shard_map/ppermute | solution.py:20
  8.1 3.4 %copy-done.2 = bf16[32,512,256]{2,1,0:T(8,128)(2,1)S(1)} copy-done((bf16[32,512,256]{2,1,0:T(8,128)(2,1)S(1)}, bf16[32,512,256]{2,1,0:T(8,128)(2,1)}, u32[]{:S(2)}) %copy-start.2) | copy-done | bytes 8388632
  11.4 1.2 %copy-done.4 = bf16[1024,512]{1,0:T(8,128)(2,1)S(1)} copy-done((bf16[1024,512]{1,0:T(8,128)(2,1)S(1)}, bf16[1024,512]{1,0:T(8,128)(2,1)}, u32[]{:S(2)}) %copy-start.4) | copy-done | bytes 1048600
  12.7 0.9 %copy-done.5 = bf16[1,8,128,128]{3,2,1,0:T(8,128)(2,1)S(1)} copy-done((bf16[1,8,128,128]{3,2,1,0:T(8,128)(2,1)S(1)}, bf16[1,8,128,128]{3,2,1,0:T(8,128)(2,1)}, u32[]{:S(2)}) %copy-start.5) | copy-done | bytes 262168
  13.6 0.7 %copy-done.7 = s32[1,8,128]{2,1,0:T(8,128)S(1)} copy-done((s32[1,8,128]{2,1,0:T(8,128)S(1)}, s32[1,8,128]{2,1,0:T(8,128)}, u32[]{:S(2)}) %copy-start.7) | copy-done | bytes 4120
  14.3 0.7 %copy-done.8 = s32[1,8,128]{2,1,0:T(8,128)S(1)} copy-done((s32[1,8,128]{2,1,0:T(8,128)S(1)}, s32[1,8,128]{2,1,0:T(8,128)}, u32[]{:S(2)}) %copy-start.8) | copy-done | bytes 4120
  15.0 0.7 %copy-done.10 = f32[1,32]{1,0:T(1,128)S(1)} copy-done((f32[1,32]{1,0:T(1,128)S(1)}, f32[1,32]{1,0:T(1,128)}, u32[]{:S(2)}) %copy-start.10) | copy-done | bytes 152
  15.7 0.7 %copy-done.11 = s32[1,8]{1,0:T(1,128)S(1)} copy-done((s32[1,8]{1,0:T(1,128)S(1)}, s32[1,8]{1,0:T(1,128)}, u32[]{:S(2)}) %copy-start.11) | copy-done | bytes 56
  16.3 7.1 %send.1 = (bf16[1024,512]{1,0:T(8,128)(2,1)S(1)}, bf16[272,256]{1,0:T(8,128)(2,1)S(1)}, bf16[272,256]{1,0:T(8,128)(2,1)S(1)}, bf16[272,256]{1,0:T(8,128)(2,1)S(1)}, bf16[272,256]{1,0:T(8,128)(2,1)S(1)}) custom-call(f32[1,32]{1,0:T(1,128)S(1)} %copy-done.10, s32[1,8]{1,0:T(1,128)S(1)} %copy-done.11, s32[1,8,128]{2,1,0:T(8,128)S(1)} %copy-done.7, ...), custom_call_target="tpu_custom_call" | custom-call | flops 6000000000 | bytes 10000000 | tf_op jit(solution)/shard_map/send/pallas_call | solution.py:95
  23.4 0.7 %collective-permute-start = (bf16[272,256]{1,0:T(8,128)(2,1)S(1)}, bf16[272,256]{1,0:T(8,128)(2,1)S(1)}, u32[]{:S(2)}, u32[]{:S(2)}) collective-permute-start(bf16[272,256]{1,0:T(8,128)(2,1)S(1)} %get-tuple-element.12), channel_id=1, source_target_pairs={{0,2},{2,0},{4,6},{6,4},{1,3},{3,1},{5,7},{7,5},{8,10},{10,8},{12,... | collective-permute-start | bytes 417800 | tf_op jit(solution)/shard_map/ppermute | solution.py:20
  24.2 3.5 %collective-permute-start.1 = (bf16[272,256]{1,0:T(8,128)(2,1)S(1)}, bf16[272,256]{1,0:T(8,128)(2,1)S(1)}, u32[]{:S(2)}, u32[]{:S(2)}) collective-permute-start(bf16[272,256]{1,0:T(8,128)(2,1)S(1)} %get-tuple-element.13), channel_id=1, source_target_pairs={{0,4},{2,6},{4,0},{6,2},{1,5},{3,7},{5,1},{7,3},{8,12},{10,14},{12... | collective-permute-start | bytes 417800 | tf_op jit(solution)/shard_map/ppermute | solution.py:20
  28.4 0.8 %collective-permute-done.10.rest_5_ = bf16[128,256]{1,0:T(8,128)(2,1)S(1)} collective-permute-done((bf16[128,256]{1,0:T(8,128)(2,1)S(1)}, bf16[128,256]{1,0:T(8,128)(2,1)S(1)}, u32[]{:S(2)}, u32[]{:S(2)}) %collective-permute-start.10) | collective-permute-done | bytes 65568 | tf_op jit(solution)/shard_map/ppermute | solution.py:20
  29.1 0.8 %collective-permute-start.15 = (bf16[128,256]{1,0:T(8,128)(2,1)S(1)}, bf16[128,256]{1,0:T(8,128)(2,1)S(1)}, u32[]{:S(2)}, u32[]{:S(2)}) collective-permute-start(bf16[128,256]{1,0:T(8,128)(2,1)S(1)} %collective-permute-done.13.rest_8_), channel_id=1, source_target_pairs={{0,16},{8,24},{16,0},{24,8},{1,17},{9,25},{17,1},{25,9},{2,18},{10... | collective-permute-start | bytes 196616 | tf_op jit(solution)/shard_map/ppermute | solution.py:20
  30.0 2.9 %collective-permute-done.11.rest_6_ = bf16[128,256]{1,0:T(8,128)(2,1)S(1)} collective-permute-done((bf16[128,256]{1,0:T(8,128)(2,1)S(1)}, bf16[128,256]{1,0:T(8,128)(2,1)S(1)}, u32[]{:S(2)}, u32[]{:S(2)}) %collective-permute-start.11) | collective-permute-done | bytes 65568 | tf_op jit(solution)/shard_map/ppermute | solution.py:20
  32.9 0.9 %collective-permute-done.15.rest_10_ = bf16[128,256]{1,0:T(8,128)(2,1)S(1)} collective-permute-done((bf16[128,256]{1,0:T(8,128)(2,1)S(1)}, bf16[128,256]{1,0:T(8,128)(2,1)S(1)}, u32[]{:S(2)}, u32[]{:S(2)}) %collective-permute-start.15) | collective-permute-done | bytes 65568 | tf_op jit(solution)/shard_map/ppermute | solution.py:20
  33.8 3.4 %collective-permute-done.19.rest_14_ = bf16[128,256]{1,0:T(8,128)(2,1)S(1)} collective-permute-done((bf16[128,256]{1,0:T(8,128)(2,1)S(1)}, bf16[128,256]{1,0:T(8,128)(2,1)S(1)}, u32[]{:S(2)}, u32[]{:S(2)}) %collective-permute-start.19) | collective-permute-done | bytes 65568 | tf_op jit(solution)/shard_map/ppermute | solution.py:20
  37.2 0.5 collective-permute-start.12
  37.7 0.5 collective-permute-done.1.refs_2_
  38.2 0.5 collective-permute-start.20
  39.3 0.6 %collective-permute-start.4 = (bf16[128,256]{1,0:T(8,128)(2,1)S(1)}, bf16[128,256]{1,0:T(8,128)(2,1)S(1)}, u32[]{:S(2)}, u32[]{:S(2)}) collective-permute-start(bf16[128,256]{1,0:T(8,128)(2,1)S(1)} %get-tuple-element.17), channel_id=1, source_target_pairs={{0,16},{8,24},{16,0},{24,8},{1,17},{9,25},{17,1},{25,9},{2,18},{10... | collective-permute-start | bytes 196616 | tf_op jit(solution)/shard_map/ppermute | solution.py:20
  39.9 1.2 %collective-permute-start.5 = (bf16[128,256]{1,0:T(8,128)(2,1)S(1)}, bf16[128,256]{1,0:T(8,128)(2,1)S(1)}, u32[]{:S(2)}, u32[]{:S(2)}) collective-permute-start(bf16[128,256]{1,0:T(8,128)(2,1)S(1)} %get-tuple-element.18), channel_id=1, source_target_pairs={{0,24},{8,16},{16,8},{24,0},{1,25},{9,17},{17,9},{25,1},{2,26},{10... | collective-permute-start | bytes 196616 | tf_op jit(solution)/shard_map/ppermute | solution.py:20
  41.1 3.6 %grad.1 = f32[1,128]{1,0:T(1,128)S(1)} custom-call(s32[1,8,128]{2,1,0:T(8,128)S(1)} %copy-done.9, bf16[1024,512]{1,0:T(8,128)(2,1)S(1)} %get-tuple-element.19.messages, bf16[32,512,256]{2,1,0:T(8,128)(2,1)S(1)} %copy-done.3, bf16[128,256]{1,0:T(8,128)(2,1)S(1)} %copy-done.6, bf16[128,256]{1,0:T(8,128)(2,1)S(1)} %collective-permute-done.6.rest_1_, ...), custom_call_target="tpu_custom_call" | custom-call | flops 4000000000 | bytes 10000000 | tf_op jit(solution)/shard_map/grad/pallas_call | solution.py:177
  44.7 1.6 %collective-permute-start.21 = (f32[1,128]{1,0:T(1,128)S(1)}, f32[1,128]{1,0:T(1,128)S(1)}, u32[]{:S(2)}, u32[]{:S(2)}) collective-permute-start(f32[1,128]{1,0:T(1,128)S(1)} %grad.1), channel_id=1, source_target_pairs={{0,1},{1,0},{2,3},{3,2},{4,5},{5,4},{6,7},{7,6},{8,9},{9,8},{10,11... | collective-permute-start | bytes 1544 | tf_op jit(solution)/shard_map/ppermute | solution.py:20
  46.3 2.0 %collective-permute-done.21 = f32[1,128]{1,0:T(1,128)S(1)} collective-permute-done((f32[1,128]{1,0:T(1,128)S(1)}, f32[1,128]{1,0:T(1,128)S(1)}, u32[]{:S(2)}, u32[]{:S(2)}) %collective-permute-start.21) | collective-permute-done | bytes 544 | tf_op jit(solution)/shard_map/ppermute | solution.py:20
  48.4 2.7 %collective-permute-start.22 = (f32[1,128]{1,0:T(1,128)S(1)}, f32[1,128]{1,0:T(1,128)S(1)}, u32[]{:S(2)}, u32[]{:S(2)}) collective-permute-start(f32[1,128]{1,0:T(1,128)S(1)} %add.9), channel_id=1, source_target_pairs={{0,2},{2,0},{4,6},{6,4},{1,3},{3,1},{5,7},{7,5},{8,10},{10,8},{12,... | collective-permute-start | bytes 1544 | tf_op jit(solution)/shard_map/ppermute | solution.py:20
  51.0 1.5 %collective-permute-done.22 = f32[1,128]{1,0:T(1,128)S(1)} collective-permute-done((f32[1,128]{1,0:T(1,128)S(1)}, f32[1,128]{1,0:T(1,128)S(1)}, u32[]{:S(2)}, u32[]{:S(2)}) %collective-permute-start.22) | collective-permute-done | bytes 544 | tf_op jit(solution)/shard_map/ppermute | solution.py:20
  52.6 3.0 %collective-permute-start.23 = (f32[1,128]{1,0:T(1,128)S(1)}, f32[1,128]{1,0:T(1,128)S(1)}, u32[]{:S(2)}, u32[]{:S(2)}) collective-permute-start(f32[1,128]{1,0:T(1,128)S(1)} %add.10), channel_id=1, source_target_pairs={{0,4},{2,6},{4,0},{6,2},{1,5},{3,7},{5,1},{7,3},{8,12},{10,14},{12... | collective-permute-start | bytes 1544 | tf_op jit(solution)/shard_map/ppermute | solution.py:20
  55.6 1.5 %collective-permute-done.23 = f32[1,128]{1,0:T(1,128)S(1)} collective-permute-done((f32[1,128]{1,0:T(1,128)S(1)}, f32[1,128]{1,0:T(1,128)S(1)}, u32[]{:S(2)}, u32[]{:S(2)}) %collective-permute-start.23) | collective-permute-done | bytes 544 | tf_op jit(solution)/shard_map/ppermute | solution.py:20
  57.1 0.5 add.11
  57.7 1.2 %finish.1 = bf16[128,256]{1,0:T(8,128)(2,1)} custom-call(s32[4]{0:T(128)S(1)} %copy-done.1, f32[4,256]{1,0:T(4,128)S(1)} %copy-done, f32[128,256]{1,0:T(8,128)S(1)} %get-tuple-element.15.refs_0_, bf16[128,256]{1,0:T(8,128)(2,1)S(1)} %collective-permute-done.3.refs_1_, bf16[128,256]{1,0:T(8,128)(2,1)S(1)} %collective-permute-done.4.refs_2_, ...), custom_call_target="tpu_custom_call" | custom-call | tf_op jit(solution)/shard_map/finish/pallas_call | solution.py:262
  (47 shorter events, 1.6 us)
Async XLA Ops:
  0.6 7.4 %collective-permute-start.7 = (bf16[128,256]{1,0:T(8,128)(2,1)}, bf16[128,256]{1,0:T(8,128)(2,1)S(1)}, u32[]{:S(2)}, u32[]{:S(2)}) collective-permute-start(bf16[128,256]{1,0:T(8,128)(2,1)} %rest_0_.1), channel_id=1, source_target_pairs={{0,16},{8,24},{16,0},{24,8},{1,17},{9,25},{17,1},{25,9},{2,18},{10... | collective-permute-start | bytes 196616 | tf_op jit(solution)/shard_map/ppermute | solution.py:20
  3.7 19.7 %collective-permute-start.6 = (bf16[128,256]{1,0:T(8,128)(2,1)}, bf16[128,256]{1,0:T(8,128)(2,1)S(1)}, u32[]{:S(2)}, u32[]{:S(2)}) collective-permute-start(bf16[128,256]{1,0:T(8,128)(2,1)} %rest_0_.1), channel_id=1, source_target_pairs={{0,8},{8,0},{16,24},{24,16},{1,9},{9,1},{17,25},{25,17},{2,10},{10... | collective-permute-start | bytes 196616 | tf_op jit(solution)/shard_map/ppermute | solution.py:20
  3.7 20.5 %collective-permute-start.9 = (bf16[128,256]{1,0:T(8,128)(2,1)}, bf16[128,256]{1,0:T(8,128)(2,1)S(1)}, u32[]{:S(2)}, u32[]{:S(2)}) collective-permute-start(bf16[128,256]{1,0:T(8,128)(2,1)} %rest_0_.1), channel_id=1, source_target_pairs={{0,2},{2,0},{4,6},{6,4},{1,3},{3,1},{5,7},{7,5},{8,10},{10,8},{12,... | collective-permute-start | bytes 196616 | tf_op jit(solution)/shard_map/ppermute | solution.py:20
  5.2 22.4 %collective-permute-start.13 = (bf16[128,256]{1,0:T(8,128)(2,1)}, bf16[128,256]{1,0:T(8,128)(2,1)S(1)}, u32[]{:S(2)}, u32[]{:S(2)}) collective-permute-start(bf16[128,256]{1,0:T(8,128)(2,1)} %rest_0_.1), channel_id=1, source_target_pairs={{0,4},{2,6},{4,0},{6,2},{1,5},{3,7},{5,1},{7,3},{8,12},{10,14},{12... | collective-permute-start | bytes 196616 | tf_op jit(solution)/shard_map/ppermute | solution.py:20
  7.8 20.0 %collective-permute-start.17 = (bf16[128,256]{1,0:T(8,128)(2,1)}, bf16[128,256]{1,0:T(8,128)(2,1)S(1)}, u32[]{:S(2)}, u32[]{:S(2)}) collective-permute-start(bf16[128,256]{1,0:T(8,128)(2,1)} %rest_0_.1), channel_id=1, source_target_pairs={{0,6},{2,4},{4,2},{6,0},{1,7},{3,5},{5,3},{7,1},{8,14},{10,12},{12... | collective-permute-start | bytes 196616 | tf_op jit(solution)/shard_map/ppermute | solution.py:20
  8.1 19.8 %collective-permute-start.8 = (bf16[128,256]{1,0:T(8,128)(2,1)S(1)}, bf16[128,256]{1,0:T(8,128)(2,1)S(1)}, u32[]{:S(2)}, u32[]{:S(2)}) collective-permute-start(bf16[128,256]{1,0:T(8,128)(2,1)S(1)} %collective-permute-done.7.rest_2_), channel_id=1, source_target_pairs={{0,8},{8,0},{16,24},{24,16},{1,9},{9,1},{17,25},{25,17},{2,10},{10... | collective-permute-start | bytes 196616 | tf_op jit(solution)/shard_map/ppermute | solution.py:20
  8.1 3.4 %copy-start.2 = (bf16[32,512,256]{2,1,0:T(8,128)(2,1)S(1)}, bf16[32,512,256]{2,1,0:T(8,128)(2,1)}, u32[]{:S(2)}) copy-start(bf16[32,512,256]{2,1,0:T(8,128)(2,1)} %basis.3) | copy-start | bytes 25165828
  11.4 1.2 %copy-start.4 = (bf16[1024,512]{1,0:T(8,128)(2,1)S(1)}, bf16[1024,512]{1,0:T(8,128)(2,1)}, u32[]{:S(2)}) copy-start(bf16[1024,512]{1,0:T(8,128)(2,1)} %table.1) | copy-start | bytes 3145732
  12.7 0.9 %copy-start.5 = (bf16[1,8,128,128]{3,2,1,0:T(8,128)(2,1)S(1)}, bf16[1,8,128,128]{3,2,1,0:T(8,128)(2,1)}, u32[]{:S(2)}) copy-start(bf16[1,8,128,128]{3,2,1,0:T(8,128)(2,1)} %weights.1) | copy-start | bytes 786436
  16.3 24.8 %copy-start.3 = (bf16[32,512,256]{2,1,0:T(8,128)(2,1)S(1)}, bf16[32,512,256]{2,1,0:T(8,128)(2,1)}, u32[]{:S(2)}) copy-start(bf16[32,512,256]{2,1,0:T(8,128)(2,1)} %basis.3) | copy-start | bytes 25165828
  16.3 24.8 %copy-start.6 = (bf16[128,256]{1,0:T(8,128)(2,1)S(1)}, bf16[128,256]{1,0:T(8,128)(2,1)}, u32[]{:S(2)}) copy-start(bf16[128,256]{1,0:T(8,128)(2,1)} %rest_0_.1) | copy-start | bytes 196612
  16.3 24.8 %copy-start.9 = (s32[1,8,128]{2,1,0:T(8,128)S(1)}, s32[1,8,128]{2,1,0:T(8,128)}, u32[]{:S(2)}) copy-start(s32[1,8,128]{2,1,0:T(8,128)} %dst.3) | copy-start | bytes 12292
  23.4 13.8 %collective-permute-start = (bf16[272,256]{1,0:T(8,128)(2,1)S(1)}, bf16[272,256]{1,0:T(8,128)(2,1)S(1)}, u32[]{:S(2)}, u32[]{:S(2)}) collective-permute-start(bf16[272,256]{1,0:T(8,128)(2,1)S(1)} %get-tuple-element.12), channel_id=1, source_target_pairs={{0,2},{2,0},{4,6},{6,4},{1,3},{3,1},{5,7},{7,5},{8,10},{10,8},{12,... | collective-permute-start | bytes 417800 | tf_op jit(solution)/shard_map/ppermute | solution.py:20
  24.2 14.0 %collective-permute-start.1 = (bf16[272,256]{1,0:T(8,128)(2,1)S(1)}, bf16[272,256]{1,0:T(8,128)(2,1)S(1)}, u32[]{:S(2)}, u32[]{:S(2)}) collective-permute-start(bf16[272,256]{1,0:T(8,128)(2,1)S(1)} %get-tuple-element.13), channel_id=1, source_target_pairs={{0,4},{2,6},{4,0},{6,2},{1,5},{3,7},{5,1},{7,3},{8,12},{10,14},{12... | collective-permute-start | bytes 417800 | tf_op jit(solution)/shard_map/ppermute | solution.py:20
  27.6 10.5 %collective-permute-start.2 = (bf16[272,256]{1,0:T(8,128)(2,1)S(1)}, bf16[272,256]{1,0:T(8,128)(2,1)S(1)}, u32[]{:S(2)}, u32[]{:S(2)}) collective-permute-start(bf16[272,256]{1,0:T(8,128)(2,1)S(1)} %get-tuple-element.14), channel_id=1, source_target_pairs={{0,6},{2,4},{4,2},{6,0},{1,7},{3,5},{5,3},{7,1},{8,14},{10,12},{12... | collective-permute-start | bytes 417800 | tf_op jit(solution)/shard_map/ppermute | solution.py:20
  27.9 1.3 %collective-permute-start.10 = (bf16[128,256]{1,0:T(8,128)(2,1)S(1)}, bf16[128,256]{1,0:T(8,128)(2,1)S(1)}, u32[]{:S(2)}, u32[]{:S(2)}) collective-permute-start(bf16[128,256]{1,0:T(8,128)(2,1)S(1)} %collective-permute-done.9.rest_4_), channel_id=1, source_target_pairs={{0,8},{8,0},{16,24},{24,16},{1,9},{9,1},{17,25},{25,17},{2,10},{10... | collective-permute-start | bytes 196616 | tf_op jit(solution)/shard_map/ppermute | solution.py:20
  27.9 5.0 %collective-permute-start.11 = (bf16[128,256]{1,0:T(8,128)(2,1)S(1)}, bf16[128,256]{1,0:T(8,128)(2,1)S(1)}, u32[]{:S(2)}, u32[]{:S(2)}) collective-permute-start(bf16[128,256]{1,0:T(8,128)(2,1)S(1)} %collective-permute-done.9.rest_4_), channel_id=1, source_target_pairs={{0,16},{8,24},{16,0},{24,8},{1,17},{9,25},{17,1},{25,9},{2,18},{10... | collective-permute-start | bytes 196616 | tf_op jit(solution)/shard_map/ppermute | solution.py:20
  29.1 4.7 %collective-permute-start.15 = (bf16[128,256]{1,0:T(8,128)(2,1)S(1)}, bf16[128,256]{1,0:T(8,128)(2,1)S(1)}, u32[]{:S(2)}, u32[]{:S(2)}) collective-permute-start(bf16[128,256]{1,0:T(8,128)(2,1)S(1)} %collective-permute-done.13.rest_8_), channel_id=1, source_target_pairs={{0,16},{8,24},{16,0},{24,8},{1,17},{9,25},{17,1},{25,9},{2,18},{10... | collective-permute-start | bytes 196616 | tf_op jit(solution)/shard_map/ppermute | solution.py:20
  32.9 4.3 %collective-permute-start.19 = (bf16[128,256]{1,0:T(8,128)(2,1)S(1)}, bf16[128,256]{1,0:T(8,128)(2,1)S(1)}, u32[]{:S(2)}, u32[]{:S(2)}) collective-permute-start(bf16[128,256]{1,0:T(8,128)(2,1)S(1)} %collective-permute-done.17.rest_12_), channel_id=1, source_target_pairs={{0,16},{8,24},{16,0},{24,8},{1,17},{9,25},{17,1},{25,9},{2,18},{10... | collective-permute-start | bytes 196616 | tf_op jit(solution)/shard_map/ppermute | solution.py:20
  33.8 5.4 %collective-permute-start.14 = (bf16[128,256]{1,0:T(8,128)(2,1)S(1)}, bf16[128,256]{1,0:T(8,128)(2,1)S(1)}, u32[]{:S(2)}, u32[]{:S(2)}) collective-permute-start(bf16[128,256]{1,0:T(8,128)(2,1)S(1)} %collective-permute-done.13.rest_8_), channel_id=1, source_target_pairs={{0,8},{8,0},{16,24},{24,16},{1,9},{9,1},{17,25},{25,17},{2,10},{10... | collective-permute-start | bytes 196616 | tf_op jit(solution)/shard_map/ppermute | solution.py:20
  37.2 2.1 %collective-permute-start.18 = (bf16[128,256]{1,0:T(8,128)(2,1)S(1)}, bf16[128,256]{1,0:T(8,128)(2,1)S(1)}, u32[]{:S(2)}, u32[]{:S(2)}) collective-permute-start(bf16[128,256]{1,0:T(8,128)(2,1)S(1)} %collective-permute-done.17.rest_12_), channel_id=1, source_target_pairs={{0,8},{8,0},{16,24},{24,16},{1,9},{9,1},{17,25},{25,17},{2,10},{10... | collective-permute-start | bytes 196616 | tf_op jit(solution)/shard_map/ppermute | solution.py:20
  37.2 2.7 %collective-permute-start.12 = (bf16[128,256]{1,0:T(8,128)(2,1)S(1)}, bf16[128,256]{1,0:T(8,128)(2,1)S(1)}, u32[]{:S(2)}, u32[]{:S(2)}) collective-permute-start(bf16[128,256]{1,0:T(8,128)(2,1)S(1)} %collective-permute-done.11.rest_6_), channel_id=1, source_target_pairs={{0,8},{8,0},{16,24},{24,16},{1,9},{9,1},{17,25},{25,17},{2,10},{10... | collective-permute-start | bytes 196616 | tf_op jit(solution)/shard_map/ppermute | solution.py:20
  38.2 2.9 %collective-permute-start.16 = (bf16[128,256]{1,0:T(8,128)(2,1)S(1)}, bf16[128,256]{1,0:T(8,128)(2,1)S(1)}, u32[]{:S(2)}, u32[]{:S(2)}) collective-permute-start(bf16[128,256]{1,0:T(8,128)(2,1)S(1)} %collective-permute-done.15.rest_10_), channel_id=1, source_target_pairs={{0,8},{8,0},{16,24},{24,16},{1,9},{9,1},{17,25},{25,17},{2,10},{10... | collective-permute-start | bytes 196616 | tf_op jit(solution)/shard_map/ppermute | solution.py:20
  38.2 2.9 %collective-permute-start.20 = (bf16[128,256]{1,0:T(8,128)(2,1)S(1)}, bf16[128,256]{1,0:T(8,128)(2,1)S(1)}, u32[]{:S(2)}, u32[]{:S(2)}) collective-permute-start(bf16[128,256]{1,0:T(8,128)(2,1)S(1)} %collective-permute-done.19.rest_14_), channel_id=1, source_target_pairs={{0,8},{8,0},{16,24},{24,16},{1,9},{9,1},{17,25},{25,17},{2,10},{10... | collective-permute-start | bytes 196616 | tf_op jit(solution)/shard_map/ppermute | solution.py:20
  38.7 19.0 %copy-start = (f32[4,256]{1,0:T(4,128)S(1)}, f32[4,256]{1,0:T(4,128)}, u32[]{:S(2)}) copy-start(f32[4,256]{1,0:T(4,128)} %bias.1) | copy-start | bytes 12292
  38.7 19.0 %copy-start.1 = (s32[4]{0:T(128)S(1)}, s32[4]{0:T(128)}, u32[]{:S(2)}) copy-start(s32[4]{0:T(128)} %type_rows.1) | copy-start | bytes 52
  39.2 18.5 %collective-permute-start.3 = (bf16[128,256]{1,0:T(8,128)(2,1)S(1)}, bf16[128,256]{1,0:T(8,128)(2,1)S(1)}, u32[]{:S(2)}, u32[]{:S(2)}) collective-permute-start(bf16[128,256]{1,0:T(8,128)(2,1)S(1)} %get-tuple-element.16), channel_id=1, source_target_pairs={{0,8},{8,0},{16,24},{24,16},{1,9},{9,1},{17,25},{25,17},{2,10},{10... | collective-permute-start | bytes 196616 | tf_op jit(solution)/shard_map/ppermute | solution.py:20
  39.3 18.4 %collective-permute-start.4 = (bf16[128,256]{1,0:T(8,128)(2,1)S(1)}, bf16[128,256]{1,0:T(8,128)(2,1)S(1)}, u32[]{:S(2)}, u32[]{:S(2)}) collective-permute-start(bf16[128,256]{1,0:T(8,128)(2,1)S(1)} %get-tuple-element.17), channel_id=1, source_target_pairs={{0,16},{8,24},{16,0},{24,8},{1,17},{9,25},{17,1},{25,9},{2,18},{10... | collective-permute-start | bytes 196616 | tf_op jit(solution)/shard_map/ppermute | solution.py:20
  39.9 17.8 %collective-permute-start.5 = (bf16[128,256]{1,0:T(8,128)(2,1)S(1)}, bf16[128,256]{1,0:T(8,128)(2,1)S(1)}, u32[]{:S(2)}, u32[]{:S(2)}) collective-permute-start(bf16[128,256]{1,0:T(8,128)(2,1)S(1)} %get-tuple-element.18), channel_id=1, source_target_pairs={{0,24},{8,16},{16,8},{24,0},{1,25},{9,17},{17,9},{25,1},{2,26},{10... | collective-permute-start | bytes 196616 | tf_op jit(solution)/shard_map/ppermute | solution.py:20
  44.7 3.6 %collective-permute-start.21 = (f32[1,128]{1,0:T(1,128)S(1)}, f32[1,128]{1,0:T(1,128)S(1)}, u32[]{:S(2)}, u32[]{:S(2)}) collective-permute-start(f32[1,128]{1,0:T(1,128)S(1)} %grad.1), channel_id=1, source_target_pairs={{0,1},{1,0},{2,3},{3,2},{4,5},{5,4},{6,7},{7,6},{8,9},{9,8},{10,11... | collective-permute-start | bytes 1544 | tf_op jit(solution)/shard_map/ppermute | solution.py:20
  48.4 4.2 %collective-permute-start.22 = (f32[1,128]{1,0:T(1,128)S(1)}, f32[1,128]{1,0:T(1,128)S(1)}, u32[]{:S(2)}, u32[]{:S(2)}) collective-permute-start(f32[1,128]{1,0:T(1,128)S(1)} %add.9), channel_id=1, source_target_pairs={{0,2},{2,0},{4,6},{6,4},{1,3},{3,1},{5,7},{7,5},{8,10},{10,8},{12,... | collective-permute-start | bytes 1544 | tf_op jit(solution)/shard_map/ppermute | solution.py:20
  52.6 4.6 %collective-permute-start.23 = (f32[1,128]{1,0:T(1,128)S(1)}, f32[1,128]{1,0:T(1,128)S(1)}, u32[]{:S(2)}, u32[]{:S(2)}) collective-permute-start(f32[1,128]{1,0:T(1,128)S(1)} %add.10), channel_id=1, source_target_pairs={{0,4},{2,6},{4,0},{6,2},{1,5},{3,7},{5,1},{7,3},{8,12},{10,14},{12... | collective-permute-start | bytes 1544 | tf_op jit(solution)/shard_map/ppermute | solution.py:20
  (4 other events, 2.7 us)

commit v2 on v0

v2 whole, which is shorter than its diff:
```python
import functools
import jax
import jax.numpy as jnp
from jax import lax
from jax.experimental import pallas as pl
from jax.experimental.pallas import tpu as pltpu
from jax.sharding import PartitionSpec as P


f32, bf16, i32 = jnp.float32, jnp.bfloat16, jnp.int32
LIMIT = 40 * 1024 * 1024
FIRST_FLOPS = 20_000_000_000
CONTRACT_ROWS = (((0,), (0,)), ((), ()))


def whole(space=pltpu.VMEM):
    return pl.BlockSpec(memory_space=space)


def spread_rows(row, rows):
    return jnp.broadcast_to(row, (rows, rows)).T


def one_hot(column, width):
    rows, lanes = column.shape
    lane = lax.broadcasted_iota(i32, (rows, lanes), 1)
    parts = [(column == lane + c).astype(bf16) for c in range(0, width, lanes)]
    return jnp.concatenate(parts, axis=1)


def send_kernel(
    n_dst, coef, mask, src_v, dst_v, table_v, weights_v, kept, _, messages, *rest
):
    outs = rest[:n_dst]
    (acc,) = rest[n_dst:]
    count, features, cols = kept.shape
    blocks, block = src_v.shape[1:]
    per_owner = blocks // n_dst
    span = per_owner * block
    size = 4

    columns = [spread_rows(src_v[0, k : k + 1, :], block) for k in range(blocks)]
    picks = jnp.concatenate([one_hot(c, table_v.shape[0]) for c in columns], axis=0)
    picked = jnp.dot(picks, table_v[...], preferred_element_type=f32).astype(bf16)
    for k in range(blocks):
        scaled = weights_v[0, k] * mask[0, k].astype(f32).astype(bf16)
        messages[k * block : (k + 1) * block, :] = jnp.dot(
            scaled, picked[k * block : (k + 1) * block, :], preferred_element_type=f32
        ).astype(bf16)

    acc[...] = jnp.zeros_like(acc)

    def mix(g, _):
        factors = [coef[0, g * size + b] for b in range(size)]
        chunk = 32
        for start in range(0, features, chunk):
            part = pl.ds(start, chunk)
            total = acc[part, :]
            for b in range(size):
                total = total + factors[b] * kept[g * size + b, part, :].astype(f32)
            acc[part, :] = total
        return 0

    lax.fori_loop(0, count // size, mix, 0)
    weight = acc[...].astype(bf16)

    me = lax.axis_index("dst")
    for d in range(n_dst):
        owner = me ^ d
        mine = messages[pl.ds(pl.multiple_of(owner * span, span), span), :]
        outs[d][:span, :] = jnp.dot(mine, weight, preferred_element_type=f32).astype(bf16)
        pad = outs[d].shape[0] - span
        which = lax.broadcasted_iota(i32, (pad, block), 0)
        slots = jnp.zeros((pad, block), i32)
        for b in range(per_owner):
            ids = dst_v[0, pl.ds(owner * per_owner + b, 1), :]
            slots = jnp.where(which == 2 * b, ids & 255, slots)
            slots = jnp.where(which == 2 * b + 1, ids >> 8, slots)
        outs[d][span:, :block] = slots.astype(f32).astype(bf16)
        outs[d][span:, block:] = jnp.zeros((pad, cols - block), bf16)


def send(coef, mask, src, dst, table, weights, basis, after, n_dst):
    _, features, cols = basis.shape
    blocks, block = src.shape[1:]
    span = blocks // n_dst * block
    pad = -(-2 * (blocks // n_dst) // 16) * 16
    return pl.pallas_call(
        functools.partial(send_kernel, n_dst),
        in_specs=[whole(pltpu.SMEM)] * 2 + [whole()] * 5 + [whole(pl.ANY)],
        out_shape=[
            jax.ShapeDtypeStruct((blocks * block, features), bf16),
        ]
        + [jax.ShapeDtypeStruct((span + pad, cols), bf16)] * n_dst,
        out_specs=[whole()] * (1 + n_dst),
        scratch_shapes=[
            pltpu.VMEM((features, cols), f32),
        ],
        compiler_params=pltpu.CompilerParams(vmem_limit_bytes=LIMIT),
        cost_estimate=pl.CostEstimate(flops=6_000_000_000, bytes_accessed=10_000_000, transcendentals=0),
        name="send",
    )(coef, mask, src, dst, table, weights, basis, after)


def first_kernel(out):
    out[...] = jnp.zeros_like(out)


def first():
    return pl.pallas_call(
        first_kernel,
        out_shape=jax.ShapeDtypeStruct((8, 128), f32),
        out_specs=whole(),
        compiler_params=pltpu.CompilerParams(vmem_limit_bytes=LIMIT),
        cost_estimate=pl.CostEstimate(flops=FIRST_FLOPS, bytes_accessed=4096, transcendentals=0),
        name="first",
    )()


def stack_kernel(type_rows, bias, _, *refs):
    parts, out, added = refs[:-2], refs[-2], refs[-1]
    rows_dev, cols = added.shape
    for d, part in enumerate(parts):
        out[d * rows_dev : (d + 1) * rows_dev, :] = part[...]
    row = lax.broadcasted_iota(i32, (rows_dev, cols), 0) + lax.axis_index("rel") * rows_dev
    total = jnp.broadcast_to(bias[0:1, :], (rows_dev, cols))
    bound = 0
    for c in range(bias.shape[0] - 1):
        bound = bound + type_rows[c]
        total = jnp.where(row >= bound, bias[c + 1 : c + 2, :], total)
    added[...] = total


def stack(type_rows, bias, after, parts):
    rows_dev, cols = parts[0].shape
    return pl.pallas_call(
        stack_kernel,
        in_specs=[whole(pltpu.SMEM), whole(), whole(pl.ANY)] + [whole()] * len(parts),
        out_shape=[
            jax.ShapeDtypeStruct((len(parts) * rows_dev, cols), bf16),
            jax.ShapeDtypeStruct((rows_dev, cols), f32),
        ],
        out_specs=[whole()] * 2,
        compiler_params=pltpu.CompilerParams(vmem_limit_bytes=LIMIT),
        name="stack",
    )(type_rows, bias, after, *parts)


def grad_kernel(n_rel, n_dst, dst, messages, basis, *rest):
    stacks, out = rest[:n_rel], rest[n_rel]
    outer, sums = rest[n_rel + 1 :]
    count, features, cols = basis.shape
    blocks, block = dst.shape[1:]
    rows_dev = stacks[0].shape[0] // n_dst
    span = blocks // n_dst * block
    rel, me = lax.axis_index("rel"), lax.axis_index("dst")

    total = None
    for d in range(n_dst):
        owner = me ^ d
        wanted = None
        columns = [
            spread_rows(dst[0, pl.ds(owner * (span // block) + b, 1), :], block)
            for b in range(span // block)
        ]
        for e in range(n_rel):
            first = (rel ^ e) * rows_dev
            picks = jnp.concatenate([one_hot(c - first, rows_dev) for c in columns], axis=0)
            more = jnp.dot(
                picks, stacks[e][d * rows_dev : (d + 1) * rows_dev, :], preferred_element_type=f32
            )
            wanted = more if wanted is None else wanted + more
        more = lax.dot_general(
            messages[pl.ds(pl.multiple_of(owner * span, span), span), :],
            wanted.astype(bf16),
            CONTRACT_ROWS,
            preferred_element_type=f32,
        )
        total = more if total is None else total + more
    outer[...] = total

    size = 4

    def contract(g, _):
        totals = [jnp.zeros((8, 128), f32)] * size
        for start in range(0, features, 16):
            part = pl.ds(start, 16)
            side = outer[part, :]
            for b in range(size):
                prod = basis[g * size + b, part, :].astype(f32) * side
                more = prod[:8, :] + prod[8:, :]
                for c in range(0, cols, 128):
                    totals[b] = totals[b] + more[:, c : c + 128]
        for b in range(size):
            sums[pl.ds(g * size + b, 1), :] = jnp.sum(totals[b], axis=0, keepdims=True)
        return 0

    lax.fori_loop(0, count // size, contract, 0)
    out[...] = jnp.sum(sums[...].T, axis=0, keepdims=True)


def grad(dst, messages, basis, stacks, n_dst):
    _, features, cols = basis.shape
    return pl.pallas_call(
        functools.partial(grad_kernel, len(stacks), n_dst),
        in_specs=[whole()] * (3 + len(stacks)),
        out_shape=jax.ShapeDtypeStruct((1, 128), f32),
        out_specs=whole(),
        scratch_shapes=[pltpu.VMEM((features, cols), f32), pltpu.VMEM((128, 128), f32)],
        compiler_params=pltpu.CompilerParams(vmem_limit_bytes=LIMIT),
        cost_estimate=pl.CostEstimate(flops=4_000_000_000, bytes_accessed=10_000_000, transcendentals=0),
        name="grad",
    )(dst, messages, basis, *stacks)


def gather_kernel(n_rel, n_dst, block, added, *refs):
    got, outs = refs[:n_dst], refs[n_dst:]
    rows_dev = outs[0].shape[0]
    span = got[0].shape[0] // block * block
    rel = lax.axis_index("rel")
    ids = []
    for d in range(n_dst):
        pairs = got[d][span:, :block].astype(f32)
        ids.append(
            [
                (pairs[2 * b : 2 * b + 1] + 256.0 * pairs[2 * b + 1 : 2 * b + 2]).astype(i32)
                for b in range(span // block)
            ]
        )
    row = lax.broadcasted_iota(i32, (rows_dev, block), 0)
    for e in range(n_rel):
        place = row + (rel ^ e) * rows_dev
        total = None
        for d in range(n_dst):
            picks = jnp.concatenate(
                [(place == one).astype(bf16) for one in ids[d]], axis=1
            )
            more = jnp.dot(picks, got[d][:span, :], preferred_element_type=f32)
            total = more if total is None else total + more
        if e == 0:
            total = total + added[...]
        outs[e][...] = total.astype(outs[e].dtype)


def gather(added, got, n_rel, block, rows_dev):
    n_dst, cols = len(got), got[0].shape[1]
    return pl.pallas_call(
        functools.partial(gather_kernel, n_rel, n_dst, block),
        in_specs=[whole()] * (1 + n_dst),
        out_shape=[
            jax.ShapeDtypeStruct((rows_dev, cols), f32 if e == 0 else bf16)
            for e in range(n_rel)
        ],
        out_specs=[whole()] * n_rel,
        compiler_params=pltpu.CompilerParams(vmem_limit_bytes=LIMIT),
        cost_estimate=pl.CostEstimate(flops=600_000_000, bytes_accessed=1_000_000, transcendentals=0),
        name="gather",
    )(added, *got)


def finish_kernel(*refs):
    parts, out = refs[:-1], refs[-1]
    total = parts[0][...]
    for part in parts[1:]:
        total = total + part[...].astype(f32)
    out[...] = total.astype(out.dtype)


def finish(parts):
    return pl.pallas_call(
        finish_kernel,
        in_specs=[whole()] * len(parts),
        out_shape=jax.ShapeDtypeStruct(parts[0].shape, bf16),
        out_specs=whole(),
        compiler_params=pltpu.CompilerParams(vmem_limit_bytes=LIMIT),
        name="finish",
    )(*parts)


def on_device(
    node_table,
    edge_weights,
    src_ids,
    dst_ids,
    block_mask,
    basis_coef,
    basis_mats,
    type_bias,
    type_rows,
    cotangent,
):
    n_rel, n_dst, n_mp = (lax.axis_size(a) for a in ("rel", "dst", "mp"))
    block = edge_weights.shape[-1]
    rows_dev = cotangent.shape[0]

    def swap(x, axis, d):
        n = lax.axis_size(axis)
        return lax.ppermute(x, axis, [(i, i ^ d) for i in range(n)])

    along = [cotangent] + [swap(cotangent, "dst", d) for d in range(1, n_dst)]
    begun = first()
    messages, *queues = send(
        basis_coef,
        block_mask,
        src_ids,
        dst_ids,
        node_table,
        edge_weights,
        basis_mats,
        begun,
        n_dst,
    )
    got = [queues[0]] + [swap(queues[d], "dst", d) for d in range(1, n_dst)]

    stacked, added = stack(type_rows, type_bias, messages, along)
    stacks = [None] * n_rel
    for e in range(0, n_rel, 2):
        stacks[e] = swap(stacked, "rel", e) if e else stacked
        stacks[e + 1] = swap(stacks[e], "rel", 1)
    partial = grad(dst_ids, messages, basis_mats, stacks, n_dst)

    sums = gather(added, got, n_rel, block, rows_dev)
    parts = [sums[0]] + [swap(sums[e], "rel", e) for e in range(1, n_rel)]
    layer_out = finish(parts)

    for axis, size in (("mp", n_mp), ("dst", n_dst)):
        d = 1
        while d < size:
            partial = partial + swap(partial, axis, d)
            d *= 2
    return layer_out, partial[:, : basis_coef.shape[1]]


def solution(mesh):
    in_specs = (
        P(("rel", "dst"), None),
        P("rel", "dst", None, None),
        P("rel", "dst", None),
        P("rel", "dst", None),
        P("rel", "dst"),
        P("rel", None),
        P(None, None, "mp"),
        P(None, "mp"),
        P(),
        P(("rel", "dst"), "mp"),
    )
    out_specs = (P(("rel", "dst"), "mp"), P("rel", None))

    return jax.shard_map(
        on_device, mesh=mesh, in_specs=in_specs, out_specs=out_specs, check_vma=False
    )
```

time: 98.9 us -> 54.1 us (0.55)
  matrix products: 32.8 us -> 0 us
  blocking collectives: 25.8 us -> 0 us
  waiting for transfers between devices: 7.93 us -> 21.3 us
  between operations: 14.1 us -> 0.83 us
  starting transfers between devices: 11.6 us -> 21.8 us
  Pallas kernels: 0 us -> 9.47 us
  local copies, waits for them, and re-layouts: 3.99 us -> 0.05 us
  other arithmetic: 2.32 us -> 0.52 us
    dot_general x6 -> x0, matrix products: 32.8 us -> none  [the longest x1 14.9 us: on_device(): jnp.dot(basis_flat, outer_sum.reshape(-1), precision=highest)]
    ppermute x0 -> x15, starting transfers between devices: none -> 21.8 us  [swap(): return lax.ppermute(x, axis, [(i, i ^ d) for i in range(n)])]
    ppermute x0 -> x15, waiting for transfers between devices: none -> 21.3 us  [swap(): return lax.ppermute(x, axis, [(i, i ^ d) for i in range(n)])]
    psum x1 -> x0, blocking collectives: 20 us -> none  [on_device(): basis_grads = lax.psum(partial_value, ('dst', 'mp'))]
    all_to_all x2 -> x0, starting transfers between devices: 11.6 us -> none  [the longest x1 6.49 us: on_device(): lax.all_to_all(slot_local, 'dst', split_axis=0, concat_axis=0, tiled=True)]
    pallas_call x0 -> x6, Pallas kernels: none -> 9.47 us  [the longest x1 4.27 us: send(): pl.pallas_call(functools.partial(send_kernel, n_dst), in_specs=[whole(plt...]
    all_to_all x2 -> x0, waiting for transfers between devices: 7.92 us -> none  [the longest x1 7.91 us: on_device(): lax.all_to_all(messages, 'dst', split_axis=0, concat_axis=0, tiled=True)]
    all_gather x1 -> x0, blocking collectives: 5.78 us -> none  [on_device(): owner_grad = lax.all_gather(cotangent, 'rel', axis=0, tiled=True)]
  transfers between devices with their start and end apart: 3 -> 15, of which waited for: 1 -> 7; matrix products, arithmetic and copies ran while one was open for 36% -> 0% of each run, Pallas kernels for 0% -> 9%
where the time goes in v2:
time: 54.1 us; the launch traced here: 53.9 us
  starting transfers between devices  21.8 us (40%)
  waiting for transfers between devices  21.3 us (39%)
  Pallas kernels  9.47 us (18%)
  between operations  0.83 us (2%)
    ppermute x15, starting transfers between devices, swap(): return lax.ppermute(x, axis, [(i, i ^ d) for i in range(n)])  21.8 us
    ppermute x15, waiting for transfers between devices, swap(): return lax.ppermute(x, axis, [(i, i ^ d) for i in range(n)])  21.3 us
    pallas_call x1, Pallas kernels, send(): pl.pallas_call(functools.partial(send_kernel, n_dst), in_specs=[whole(plt...  4.27 us
    pallas_call x1, Pallas kernels, grad(): pl.pallas_call(functools.partial(grad_kernel, len(stacks), n_dst), in_spe...  3.49 us
  transfers between devices with their start and end apart: 15, of which 7 were waited for; matrix products, arithmetic and copies ran while one was open for 0% of the time, Pallas kernels for 9%

profile of v2, /device:TPU:0, one launch (start us, length us, event | category | flops | bytes accessed | tf_op | source)
XLA Modules:
  0.0 53.9 jit_solution(10047972885697310247)
XLA Ops:
  0.7 4.1 %collective-permute-start.1 = (bf16[128,256]{1,0:T(8,128)(2,1)}, bf16[128,256]{1,0:T(8,128)(2,1)S(1)}, u32[]{:S(2)}, u32[]{:S(2)}) collective-permute-start(bf16[128,256]{1,0:T(8,128)(2,1)} %refs_0_.1), channel_id=1, source_target_pairs={{0,4},{2,6},{4,0},{6,2},{1,5},{3,7},{5,1},{7,3},{8,12},{10,14},{12... | collective-permute-start | bytes 196616 | tf_op jit(solution)/shard_map/ppermute | solution.py:298
  4.8 1.6 %collective-permute-start = (bf16[128,256]{1,0:T(8,128)(2,1)}, bf16[128,256]{1,0:T(8,128)(2,1)S(1)}, u32[]{:S(2)}, u32[]{:S(2)}) collective-permute-start(bf16[128,256]{1,0:T(8,128)(2,1)} %refs_0_.1), channel_id=1, source_target_pairs={{0,2},{2,0},{4,6},{6,4},{1,3},{3,1},{5,7},{7,5},{8,10},{10,8},{12,... | collective-permute-start | bytes 196616 | tf_op jit(solution)/shard_map/ppermute | solution.py:298
  6.4 0.0 collective-permute-start.2
  6.5 0.0 copy-start
  6.5 0.0 copy-start.1
  6.5 0.0 copy-start.2
  6.5 4.3 %send.1 = (bf16[1024,512]{1,0:T(8,128)(2,1)S(1)}, bf16[272,256]{1,0:T(8,128)(2,1)S(1)}, bf16[272,256]{1,0:T(8,128)(2,1)S(1)}, bf16[272,256]{1,0:T(8,128)(2,1)S(1)}, bf16[272,256]{1,0:T(8,128)(2,1)S(1)}) custom-call(f32[1,32]{1,0:T(1,128)S(1)} %copy-done.8, s32[1,8]{1,0:T(1,128)S(1)} %copy-done.9, s32[1,8,128]{2,1,0:T(8,128)S(1)} %copy-done.6, ...), custom_call_target="tpu_custom_call" | custom-call | flops 6000000000 | bytes 10000000 | tf_op jit(solution)/shard_map/send/pallas_call | solution.py:88
  10.8 0.0 collective-permute-done.1.refs_2_
  10.8 1.9 %collective-permute-done.2.refs_3_ = bf16[128,256]{1,0:T(8,128)(2,1)S(1)} collective-permute-done((bf16[128,256]{1,0:T(8,128)(2,1)}, bf16[128,256]{1,0:T(8,128)(2,1)S(1)}, u32[]{:S(2)}, u32[]{:S(2)}) %collective-permute-start.2) | collective-permute-done | bytes 65568 | tf_op jit(solution)/shard_map/ppermute | solution.py:298
  12.7 0.6 %stack.1 = (bf16[512,256]{1,0:T(8,128)(2,1)S(1)}, f32[128,256]{1,0:T(8,128)S(1)}) custom-call(s32[4]{0:T(128)S(1)} %copy-done.2, f32[4,256]{1,0:T(4,128)S(1)} %copy-done.1, bf16[1024,512]{1,0:T(8,128)(2,1)S(1)} %get-tuple-element.13._.messages, bf16[128,256]{1,0:T(8,128)(2,1)S(1)} %copy-done, bf16[128,256]{1,0:T(8,128)(2,1)S(1)} %collective-permute-done.refs_1_, ...), custom_call_target="tpu_custom_call" | custom-call | tf_op jit(solution)/shard_map/stack/pallas_call | solution.py:136
  13.3 1.6 %collective-permute-start.10 = (bf16[512,256]{1,0:T(8,128)(2,1)S(1)}, bf16[512,256]{1,0:T(8,128)(2,1)S(1)}, u32[]{:S(2)}, u32[]{:S(2)}) collective-permute-start(bf16[512,256]{1,0:T(8,128)(2,1)S(1)} %get-tuple-element.23.rest_0_), channel_id=1, source_target_pairs={{0,16},{8,24},{16,0},{24,8},{1,17},{9,25},{17,1},{25,9},{2,18},{10... | collective-permute-start | bytes 786440 | tf_op jit(solution)/shard_map/ppermute | solution.py:298
  14.8 4.9 %collective-permute-done.10.rest_2_ = bf16[512,256]{1,0:T(8,128)(2,1)S(1)} collective-permute-done((bf16[512,256]{1,0:T(8,128)(2,1)S(1)}, bf16[512,256]{1,0:T(8,128)(2,1)S(1)}, u32[]{:S(2)}, u32[]{:S(2)}) %collective-permute-start.10) | collective-permute-done | bytes 262176 | tf_op jit(solution)/shard_map/ppermute | solution.py:298
  19.8 0.8 %collective-permute-start.3 = (bf16[272,256]{1,0:T(8,128)(2,1)S(1)}, bf16[272,256]{1,0:T(8,128)(2,1)S(1)}, u32[]{:S(2)}, u32[]{:S(2)}) collective-permute-start(bf16[272,256]{1,0:T(8,128)(2,1)S(1)} %get-tuple-element.16), channel_id=1, source_target_pairs={{0,2},{2,0},{4,6},{6,4},{1,3},{3,1},{5,7},{7,5},{8,10},{10,8},{12,... | collective-permute-start | bytes 417800 | tf_op jit(solution)/shard_map/ppermute | solution.py:298
  20.6 2.5 %collective-permute-start.4 = (bf16[272,256]{1,0:T(8,128)(2,1)S(1)}, bf16[272,256]{1,0:T(8,128)(2,1)S(1)}, u32[]{:S(2)}, u32[]{:S(2)}) collective-permute-start(bf16[272,256]{1,0:T(8,128)(2,1)S(1)} %get-tuple-element.17), channel_id=1, source_target_pairs={{0,4},{2,6},{4,0},{6,2},{1,5},{3,7},{5,1},{7,3},{8,12},{10,14},{12... | collective-permute-start | bytes 417800 | tf_op jit(solution)/shard_map/ppermute | solution.py:298
  23.1 1.1 %collective-permute-start.5 = (bf16[272,256]{1,0:T(8,128)(2,1)S(1)}, bf16[272,256]{1,0:T(8,128)(2,1)S(1)}, u32[]{:S(2)}, u32[]{:S(2)}) collective-permute-start(bf16[272,256]{1,0:T(8,128)(2,1)S(1)} %get-tuple-element.18), channel_id=1, source_target_pairs={{0,6},{2,4},{4,2},{6,0},{1,7},{3,5},{5,3},{7,1},{8,14},{10,12},{12... | collective-permute-start | bytes 417800 | tf_op jit(solution)/shard_map/ppermute | solution.py:298
  24.2 4.7 %collective-permute-done.3.refs_1_ = bf16[272,256]{1,0:T(8,128)(2,1)S(1)} collective-permute-done((bf16[272,256]{1,0:T(8,128)(2,1)S(1)}, bf16[272,256]{1,0:T(8,128)(2,1)S(1)}, u32[]{:S(2)}, u32[]{:S(2)}) %collective-permute-start.3) | collective-permute-done | bytes 139296 | tf_op jit(solution)/shard_map/ppermute | solution.py:298
  28.9 0.0 collective-permute-done.4.refs_2_
  28.9 5.3 %collective-permute-done.5.refs_3_ = bf16[272,256]{1,0:T(8,128)(2,1)S(1)} collective-permute-done((bf16[272,256]{1,0:T(8,128)(2,1)S(1)}, bf16[272,256]{1,0:T(8,128)(2,1)S(1)}, u32[]{:S(2)}, u32[]{:S(2)}) %collective-permute-start.5) | collective-permute-done | bytes 139296 | tf_op jit(solution)/shard_map/ppermute | solution.py:298
  34.1 0.5 gather.1
  34.6 0.1 collective-permute-start.6
  34.7 1.6 %collective-permute-start.7 = (bf16[128,256]{1,0:T(8,128)(2,1)S(1)}, bf16[128,256]{1,0:T(8,128)(2,1)S(1)}, u32[]{:S(2)}, u32[]{:S(2)}) collective-permute-start(bf16[128,256]{1,0:T(8,128)(2,1)S(1)} %get-tuple-element.21), channel_id=1, source_target_pairs={{0,16},{8,24},{16,0},{24,8},{1,17},{9,25},{17,1},{25,9},{2,18},{10... | collective-permute-start | bytes 196616 | tf_op jit(solution)/shard_map/ppermute | solution.py:298
  36.2 0.3 collective-permute-start.8
  36.5 0.0 collective-permute-done.9.rest_1_
  36.5 3.5 %grad.1 = f32[1,128]{1,0:T(1,128)S(1)} custom-call(s32[1,8,128]{2,1,0:T(8,128)S(1)} %copy-done.7, bf16[1024,512]{1,0:T(8,128)(2,1)S(1)} %get-tuple-element.13._.messages, bf16[32,512,256]{2,1,0:T(8,128)(2,1)S(1)} %copy-done.3, bf16[512,256]{1,0:T(8,128)(2,1)S(1)} %get-tuple-element.23.rest_0_, bf16[512,256]{1,0:T(8,128)(2,1)S(1)} %collective-permute-done.9.rest_1_, ...), custom_call_target="tpu_custom_call" | custom-call | flops 4000000000 | bytes 10000000 | tf_op jit(solution)/shard_map/grad/pallas_call | solution.py:204
  40.0 1.6 %collective-permute-start.12 = (f32[1,128]{1,0:T(1,128)S(1)}, f32[1,128]{1,0:T(1,128)S(1)}, u32[]{:S(2)}, u32[]{:S(2)}) collective-permute-start(f32[1,128]{1,0:T(1,128)S(1)} %grad.1), channel_id=1, source_target_pairs={{0,1},{1,0},{2,3},{3,2},{4,5},{5,4},{6,7},{7,6},{8,9},{9,8},{10,11... | collective-permute-start | bytes 1544 | tf_op jit(solution)/shard_map/ppermute | solution.py:298
  41.6 2.0 %collective-permute-done.12 = f32[1,128]{1,0:T(1,128)S(1)} collective-permute-done((f32[1,128]{1,0:T(1,128)S(1)}, f32[1,128]{1,0:T(1,128)S(1)}, u32[]{:S(2)}, u32[]{:S(2)}) %collective-permute-start.12) | collective-permute-done | bytes 544 | tf_op jit(solution)/shard_map/ppermute | solution.py:298
  43.7 2.7 %collective-permute-start.13 = (f32[1,128]{1,0:T(1,128)S(1)}, f32[1,128]{1,0:T(1,128)S(1)}, u32[]{:S(2)}, u32[]{:S(2)}) collective-permute-start(f32[1,128]{1,0:T(1,128)S(1)} %add.9), channel_id=1, source_target_pairs={{0,2},{2,0},{4,6},{6,4},{1,3},{3,1},{5,7},{7,5},{8,10},{10,8},{12,... | collective-permute-start | bytes 1544 | tf_op jit(solution)/shard_map/ppermute | solution.py:298
  46.4 1.5 %collective-permute-done.13 = f32[1,128]{1,0:T(1,128)S(1)} collective-permute-done((f32[1,128]{1,0:T(1,128)S(1)}, f32[1,128]{1,0:T(1,128)S(1)}, u32[]{:S(2)}, u32[]{:S(2)}) %collective-permute-start.13) | collective-permute-done | bytes 544 | tf_op jit(solution)/shard_map/ppermute | solution.py:298
  47.9 3.9 %collective-permute-start.14 = (f32[1,128]{1,0:T(1,128)S(1)}, f32[1,128]{1,0:T(1,128)S(1)}, u32[]{:S(2)}, u32[]{:S(2)}) collective-permute-start(f32[1,128]{1,0:T(1,128)S(1)} %add.10), channel_id=1, source_target_pairs={{0,4},{2,6},{4,0},{6,2},{1,5},{3,7},{5,1},{7,3},{8,12},{10,14},{12... | collective-permute-start | bytes 1544 | tf_op jit(solution)/shard_map/ppermute | solution.py:298
  51.9 0.7 %finish.1 = bf16[128,256]{1,0:T(8,128)(2,1)} custom-call(f32[128,256]{1,0:T(8,128)S(1)} %get-tuple-element.19.refs_0_, bf16[128,256]{1,0:T(8,128)(2,1)S(1)} %collective-permute-done.6.refs_1_, bf16[128,256]{1,0:T(8,128)(2,1)S(1)} %collective-permute-done.7.refs_2_, bf16[128,256]{1,0:T(8,128)(2,1)S(1)} %collective-permute-done.8.refs_3_), custom_call_target="tpu_custom_call" | custom-call | tf_op jit(solution)/shard_map/finish/pallas_call | solution.py:270
  52.5 0.9 %collective-permute-done.14 = f32[1,128]{1,0:T(1,128)S(1)} collective-permute-done((f32[1,128]{1,0:T(1,128)S(1)}, f32[1,128]{1,0:T(1,128)S(1)}, u32[]{:S(2)}, u32[]{:S(2)}) %collective-permute-start.14) | collective-permute-done | bytes 544 | tf_op jit(solution)/shard_map/ppermute | solution.py:298
  53.4 0.5 add.11
  (27 shorter events, 0.1 us)
Async XLA Ops:
  0.6 5.8 %copy-start.3 = (bf16[32,512,256]{2,1,0:T(8,128)(2,1)S(1)}, bf16[32,512,256]{2,1,0:T(8,128)(2,1)}, u32[]{:S(2)}) copy-start(bf16[32,512,256]{2,1,0:T(8,128)(2,1)} %basis.1) | copy-start | bytes 25165828
  0.6 5.8 %copy-start.7 = (s32[1,8,128]{2,1,0:T(8,128)S(1)}, s32[1,8,128]{2,1,0:T(8,128)}, u32[]{:S(2)}) copy-start(s32[1,8,128]{2,1,0:T(8,128)} %dst.1) | copy-start | bytes 12292
  0.7 5.8 %copy-start.8 = (f32[1,32]{1,0:T(1,128)S(1)}, f32[1,32]{1,0:T(1,128)}, u32[]{:S(2)}) copy-start(f32[1,32]{1,0:T(1,128)} %coef.1) | copy-start | bytes 388
  0.7 5.8 %copy-start.9 = (s32[1,8]{1,0:T(1,128)S(1)}, s32[1,8]{1,0:T(1,128)}, u32[]{:S(2)}) copy-start(s32[1,8]{1,0:T(1,128)} %mask.1) | copy-start | bytes 100
  0.7 5.8 %copy-start.6 = (s32[1,8,128]{2,1,0:T(8,128)S(1)}, s32[1,8,128]{2,1,0:T(8,128)}, u32[]{:S(2)}) copy-start(s32[1,8,128]{2,1,0:T(8,128)} %src_v.1) | copy-start | bytes 12292
  0.7 5.8 %copy-start.5 = (bf16[1,8,128,128]{3,2,1,0:T(8,128)(2,1)S(1)}, bf16[1,8,128,128]{3,2,1,0:T(8,128)(2,1)}, u32[]{:S(2)}) copy-start(bf16[1,8,128,128]{3,2,1,0:T(8,128)(2,1)} %weights_v.1) | copy-start | bytes 786436
  0.7 5.8 %copy-start.4 = (bf16[1024,512]{1,0:T(8,128)(2,1)S(1)}, bf16[1024,512]{1,0:T(8,128)(2,1)}, u32[]{:S(2)}) copy-start(bf16[1024,512]{1,0:T(8,128)(2,1)} %table_v.1) | copy-start | bytes 3145732
  0.7 10.1 %collective-permute-start.1 = (bf16[128,256]{1,0:T(8,128)(2,1)}, bf16[128,256]{1,0:T(8,128)(2,1)S(1)}, u32[]{:S(2)}, u32[]{:S(2)}) collective-permute-start(bf16[128,256]{1,0:T(8,128)(2,1)} %refs_0_.1), channel_id=1, source_target_pairs={{0,4},{2,6},{4,0},{6,2},{1,5},{3,7},{5,1},{7,3},{8,12},{10,14},{12... | collective-permute-start | bytes 196616 | tf_op jit(solution)/shard_map/ppermute | solution.py:298
  4.8 6.0 %collective-permute-start = (bf16[128,256]{1,0:T(8,128)(2,1)}, bf16[128,256]{1,0:T(8,128)(2,1)S(1)}, u32[]{:S(2)}, u32[]{:S(2)}) collective-permute-start(bf16[128,256]{1,0:T(8,128)(2,1)} %refs_0_.1), channel_id=1, source_target_pairs={{0,2},{2,0},{4,6},{6,4},{1,3},{3,1},{5,7},{7,5},{8,10},{10,8},{12,... | collective-permute-start | bytes 196616 | tf_op jit(solution)/shard_map/ppermute | solution.py:298
  6.4 6.3 %collective-permute-start.2 = (bf16[128,256]{1,0:T(8,128)(2,1)}, bf16[128,256]{1,0:T(8,128)(2,1)S(1)}, u32[]{:S(2)}, u32[]{:S(2)}) collective-permute-start(bf16[128,256]{1,0:T(8,128)(2,1)} %refs_0_.1), channel_id=1, source_target_pairs={{0,6},{2,4},{4,2},{6,0},{1,7},{3,5},{5,3},{7,1},{8,14},{10,12},{12... | collective-permute-start | bytes 196616 | tf_op jit(solution)/shard_map/ppermute | solution.py:298
  6.5 6.2 %copy-start = (bf16[128,256]{1,0:T(8,128)(2,1)S(1)}, bf16[128,256]{1,0:T(8,128)(2,1)}, u32[]{:S(2)}) copy-start(bf16[128,256]{1,0:T(8,128)(2,1)} %refs_0_.1) | copy-start | bytes 196612
  6.5 6.2 %copy-start.1 = (f32[4,256]{1,0:T(4,128)S(1)}, f32[4,256]{1,0:T(4,128)}, u32[]{:S(2)}) copy-start(f32[4,256]{1,0:T(4,128)} %bias.1) | copy-start | bytes 12292
  6.5 6.2 %copy-start.2 = (s32[4]{0:T(128)S(1)}, s32[4]{0:T(128)}, u32[]{:S(2)}) copy-start(s32[4]{0:T(128)} %type_rows.1) | copy-start | bytes 52
  13.3 6.5 %collective-permute-start.10 = (bf16[512,256]{1,0:T(8,128)(2,1)S(1)}, bf16[512,256]{1,0:T(8,128)(2,1)S(1)}, u32[]{:S(2)}, u32[]{:S(2)}) collective-permute-start(bf16[512,256]{1,0:T(8,128)(2,1)S(1)} %get-tuple-element.23.rest_0_), channel_id=1, source_target_pairs={{0,16},{8,24},{16,0},{24,8},{1,17},{9,25},{17,1},{25,9},{2,18},{10... | collective-permute-start | bytes 786440 | tf_op jit(solution)/shard_map/ppermute | solution.py:298
  14.8 21.7 %collective-permute-start.9 = (bf16[512,256]{1,0:T(8,128)(2,1)S(1)}, bf16[512,256]{1,0:T(8,128)(2,1)S(1)}, u32[]{:S(2)}, u32[]{:S(2)}) collective-permute-start(bf16[512,256]{1,0:T(8,128)(2,1)S(1)} %get-tuple-element.23.rest_0_), channel_id=1, source_target_pairs={{0,8},{8,0},{16,24},{24,16},{1,9},{9,1},{17,25},{25,17},{2,10},{10... | collective-permute-start | bytes 786440 | tf_op jit(solution)/shard_map/ppermute | solution.py:298
  19.8 16.8 %collective-permute-start.11 = (bf16[512,256]{1,0:T(8,128)(2,1)S(1)}, bf16[512,256]{1,0:T(8,128)(2,1)S(1)}, u32[]{:S(2)}, u32[]{:S(2)}) collective-permute-start(bf16[512,256]{1,0:T(8,128)(2,1)S(1)} %collective-permute-done.10.rest_2_), channel_id=1, source_target_pairs={{0,8},{8,0},{16,24},{24,16},{1,9},{9,1},{17,25},{25,17},{2,10},{10... | collective-permute-start | bytes 786440 | tf_op jit(solution)/shard_map/ppermute | solution.py:298
  19.8 9.1 %collective-permute-start.3 = (bf16[272,256]{1,0:T(8,128)(2,1)S(1)}, bf16[272,256]{1,0:T(8,128)(2,1)S(1)}, u32[]{:S(2)}, u32[]{:S(2)}) collective-permute-start(bf16[272,256]{1,0:T(8,128)(2,1)S(1)} %get-tuple-element.16), channel_id=1, source_target_pairs={{0,2},{2,0},{4,6},{6,4},{1,3},{3,1},{5,7},{7,5},{8,10},{10,8},{12,... | collective-permute-start | bytes 417800 | tf_op jit(solution)/shard_map/ppermute | solution.py:298
  20.6 8.3 %collective-permute-start.4 = (bf16[272,256]{1,0:T(8,128)(2,1)S(1)}, bf16[272,256]{1,0:T(8,128)(2,1)S(1)}, u32[]{:S(2)}, u32[]{:S(2)}) collective-permute-start(bf16[272,256]{1,0:T(8,128)(2,1)S(1)} %get-tuple-element.17), channel_id=1, source_target_pairs={{0,4},{2,6},{4,0},{6,2},{1,5},{3,7},{5,1},{7,3},{8,12},{10,14},{12... | collective-permute-start | bytes 417800 | tf_op jit(solution)/shard_map/ppermute | solution.py:298
  23.1 11.0 %collective-permute-start.5 = (bf16[272,256]{1,0:T(8,128)(2,1)S(1)}, bf16[272,256]{1,0:T(8,128)(2,1)S(1)}, u32[]{:S(2)}, u32[]{:S(2)}) collective-permute-start(bf16[272,256]{1,0:T(8,128)(2,1)S(1)} %get-tuple-element.18), channel_id=1, source_target_pairs={{0,6},{2,4},{4,2},{6,0},{1,7},{3,5},{5,3},{7,1},{8,14},{10,12},{12... | collective-permute-start | bytes 417800 | tf_op jit(solution)/shard_map/ppermute | solution.py:298
  34.6 17.3 %collective-permute-start.6 = (bf16[128,256]{1,0:T(8,128)(2,1)S(1)}, bf16[128,256]{1,0:T(8,128)(2,1)S(1)}, u32[]{:S(2)}, u32[]{:S(2)}) collective-permute-start(bf16[128,256]{1,0:T(8,128)(2,1)S(1)} %get-tuple-element.20), channel_id=1, source_target_pairs={{0,8},{8,0},{16,24},{24,16},{1,9},{9,1},{17,25},{25,17},{2,10},{10... | collective-permute-start | bytes 196616 | tf_op jit(solution)/shard_map/ppermute | solution.py:298
  34.7 17.2 %collective-permute-start.7 = (bf16[128,256]{1,0:T(8,128)(2,1)S(1)}, bf16[128,256]{1,0:T(8,128)(2,1)S(1)}, u32[]{:S(2)}, u32[]{:S(2)}) collective-permute-start(bf16[128,256]{1,0:T(8,128)(2,1)S(1)} %get-tuple-element.21), channel_id=1, source_target_pairs={{0,16},{8,24},{16,0},{24,8},{1,17},{9,25},{17,1},{25,9},{2,18},{10... | collective-permute-start | bytes 196616 | tf_op jit(solution)/shard_map/ppermute | solution.py:298
  36.2 15.6 %collective-permute-start.8 = (bf16[128,256]{1,0:T(8,128)(2,1)S(1)}, bf16[128,256]{1,0:T(8,128)(2,1)S(1)}, u32[]{:S(2)}, u32[]{:S(2)}) collective-permute-start(bf16[128,256]{1,0:T(8,128)(2,1)S(1)} %get-tuple-element.22), channel_id=1, source_target_pairs={{0,24},{8,16},{16,8},{24,0},{1,25},{9,17},{17,9},{25,1},{2,26},{10... | collective-permute-start | bytes 196616 | tf_op jit(solution)/shard_map/ppermute | solution.py:298
  40.0 3.6 %collective-permute-start.12 = (f32[1,128]{1,0:T(1,128)S(1)}, f32[1,128]{1,0:T(1,128)S(1)}, u32[]{:S(2)}, u32[]{:S(2)}) collective-permute-start(f32[1,128]{1,0:T(1,128)S(1)} %grad.1), channel_id=1, source_target_pairs={{0,1},{1,0},{2,3},{3,2},{4,5},{5,4},{6,7},{7,6},{8,9},{9,8},{10,11... | collective-permute-start | bytes 1544 | tf_op jit(solution)/shard_map/ppermute | solution.py:298
  43.7 4.3 %collective-permute-start.13 = (f32[1,128]{1,0:T(1,128)S(1)}, f32[1,128]{1,0:T(1,128)S(1)}, u32[]{:S(2)}, u32[]{:S(2)}) collective-permute-start(f32[1,128]{1,0:T(1,128)S(1)} %add.9), channel_id=1, source_target_pairs={{0,2},{2,0},{4,6},{6,4},{1,3},{3,1},{5,7},{7,5},{8,10},{10,8},{12,... | collective-permute-start | bytes 1544 | tf_op jit(solution)/shard_map/ppermute | solution.py:298
  47.9 5.5 %collective-permute-start.14 = (f32[1,128]{1,0:T(1,128)S(1)}, f32[1,128]{1,0:T(1,128)S(1)}, u32[]{:S(2)}, u32[]{:S(2)}) collective-permute-start(f32[1,128]{1,0:T(1,128)S(1)} %add.10), channel_id=1, source_target_pairs={{0,4},{2,6},{4,0},{6,2},{1,5},{3,7},{5,1},{7,3},{8,12},{10,14},{12... | collective-permute-start | bytes 1544 | tf_op jit(solution)/shard_map/ppermute | solution.py:298
